TPU v7x, 256 devices: a 4x2x16 block of a 4x16x16 slice. The times are simulated.
256 devices in a mesh: grp: 2 (over y), dp: 128 (over z, x, core).
Axes of the slice: x: 4, y: 2, z: 16, core: 2. Of those that a mesh axis runs over, the one named last changes fastest.
The devices are a block of a 4x16x16 slice.
Arguments:
- hidden_in: bfloat16 [2, 512, 4096], P(None, ('grp', 'dp')), parts along dimension 1, may hold values from -6 to 6
- norm_gain: float32 [4096], replicated, may hold values from 0.1 to 1.9
- queries: bfloat16 [2, 512, 4096], P(None, ('grp', 'dp')), parts along dimension 1, may hold values from -72 to 72
- new_keys: bfloat16 [2, 512, 1024], P(None, ('grp', 'dp')), parts along dimension 1, may hold values from -9 to 9
- new_values: bfloat16 [2, 512, 1024], P(None, ('grp', 'dp')), parts along dimension 1, may hold values from -6 to 6
- cache_keys: bfloat16 [512, 384, 1024], P(('grp', 'dp')), parts along dimension 0, may hold values from -9 to 9
- cache_values: bfloat16 [512, 384, 1024], P(('grp', 'dp')), parts along dimension 0, may hold values from -6 to 6
- lengths: int32 [512], P(('grp', 'dp')), parts along dimension 0, may hold values from 1 to 384
- routes: int32 [2, 512, 2], P(None, ('grp', 'dp')), parts along dimension 1, may hold values from 0 to 3, all different within a row; in each aligned block of 2 rows (0 to 1, 2 to 3, ..., all dimensions but the last counted through in order) at most 2 rows name the same one
- gate_logits: float32 [2, 512, 2], P(None, ('grp', 'dp')), parts along dimension 1, may hold values from -6 to 6
- w_gate: bfloat16 [28672, 4096], P('dp'), may hold values from -0.09375 to 0.09375
- w_up: bfloat16 [28672, 4096], P('dp'), may hold values from -0.09375 to 0.09375
- w_down: bfloat16 [28672, 4096], P('dp'), may hold values from -0.0625 to 0.0625
Outputs:
- hidden_out: bfloat16 [2, 512, 4096], P(None, ('grp', 'dp')), parts along dimension 1
There are 2 independent parts, one for each index of `grp`. A program takes and returns all parts, laid end to end along the dimension named above; an argument that names none is the same for every part. Nothing has to cross between parts.
Inputs may be any that keep to these rules, and one draw needn't show every extreme that they name: `routes`: each token names 2 different experts. Among the 2 tokens of one device at one decoded position no expert is named more than 2 times, a bound that some block reaches.
All inputs are finite; a program needn't handle non-finite values.
Results may differ from a plain program's by a relative error of at most 0.0055.
Values may be sent and summed in bfloat16 or wider, within the bound.
A program may use at most 192 MiB of HBM per device.

v0:
```python
import jax
import jax.numpy as jnp
from jax import lax
from jax.sharding import PartitionSpec as P

HEADS = 32
KV_HEADS = 8
HEAD_DIM = 128
TOP = 2
EXPERTS = 4
NEW = 2
CAP = 2


def attend(queries, new_keys, new_values, cache_keys, cache_values, lengths):
    docs = queries.shape[1]
    cache_len = cache_keys.shape[1]
    group_size = HEADS // KV_HEADS
    score_scale = HEAD_DIM ** (-0.5)
    query_heads = queries.reshape(NEW, docs, KV_HEADS, group_size, HEAD_DIM)
    keys_cache = cache_keys.reshape(docs, cache_len, KV_HEADS, HEAD_DIM)
    vals_cache = cache_values.reshape(docs, cache_len, KV_HEADS, HEAD_DIM)
    keys_fresh = new_keys.reshape(NEW, docs, KV_HEADS, HEAD_DIM)
    vals_fresh = new_values.reshape(NEW, docs, KV_HEADS, HEAD_DIM)
    scores_cache = (
        jnp.einsum("tdhgc,dshc->tdhgs", query_heads, keys_cache, preferred_element_type=jnp.float32)
        * score_scale
    )
    scores_fresh = (
        jnp.einsum("tdhgc,udhc->tdhgu", query_heads, keys_fresh, preferred_element_type=jnp.float32)
        * score_scale
    )
    positions = jnp.arange(cache_len, dtype=jnp.int32)
    in_range = positions[None, :] < lengths[:, None]
    scores_cache = jnp.where(in_range[None, :, None, None, :], scores_cache, -1e30)
    order = jnp.arange(NEW, dtype=jnp.int32)
    causal = order[None, :] <= order[:, None]
    scores_fresh = jnp.where(causal[:, None, None, None, :], scores_fresh, -1e30)
    largest = jnp.maximum(
        jnp.max(scores_cache, -1, keepdims=True), jnp.max(scores_fresh, -1, keepdims=True)
    )
    exp_cache = jnp.exp(scores_cache - largest)
    exp_fresh = jnp.exp(scores_fresh - largest)
    total = jnp.sum(exp_cache, -1, keepdims=True) + jnp.sum(exp_fresh, -1, keepdims=True)
    probs_cache = (exp_cache / total).astype(jnp.bfloat16)
    probs_fresh = (exp_fresh / total).astype(jnp.bfloat16)
    context = jnp.einsum(
        "tdhgs,dshc->tdhgc", probs_cache, vals_cache, preferred_element_type=jnp.float32
    )
    context = context + jnp.einsum(
        "tdhgu,udhc->tdhgc", probs_fresh, vals_fresh, preferred_element_type=jnp.float32
    )
    return context.reshape(NEW, docs, HEADS * HEAD_DIM)


def slot_table(route_rows):
    flat_ids = route_rows.reshape(-1)
    matches = (flat_ids[:, None] == jnp.arange(EXPERTS, dtype=jnp.int32)[None, :]).astype(jnp.int32)
    before = jnp.cumsum(matches, axis=0) - matches
    slot_ids = flat_ids * CAP + jnp.sum(before * matches, axis=1)
    slots_all = jnp.arange(EXPERTS * CAP, dtype=jnp.int32)
    return (slots_all[:, None] == slot_ids[None, :]).astype(jnp.float32)


def expert_rows(flat_rows, w_gate, w_up, w_down):
    gate_val = lax.dot_general(
        flat_rows, w_gate, (((1,), (1,)), ((), ())), preferred_element_type=jnp.float32
    )
    up_val = lax.dot_general(
        flat_rows, w_up, (((1,), (1,)), ((), ())), preferred_element_type=jnp.float32
    )
    act = (jax.nn.silu(gate_val) * up_val).astype(jnp.bfloat16)
    return jnp.dot(act, w_down, preferred_element_type=jnp.float32)


def per_device(
    hidden_in,
    norm_gain,
    queries,
    new_keys,
    new_values,
    cache_keys,
    cache_values,
    lengths,
    routes,
    gate_logits,
    w_gate,
    w_up,
    w_down,
):
    docs = hidden_in.shape[1]
    width = hidden_in.shape[2]
    context = attend(queries, new_keys, new_values, cache_keys, cache_values, lengths)
    carried = hidden_in.astype(jnp.float32) + context
    normed = (
        carried * lax.rsqrt(jnp.mean(carried * carried, -1, keepdims=True) + 1e-05) * norm_gain
    ).astype(jnp.bfloat16)
    groups = lax.axis_size("dp") // EXPERTS
    top_share = jax.nn.sigmoid(gate_logits[..., 0] - gate_logits[..., 1])
    shares = jnp.stack([top_share, 1.0 - top_share], axis=-1)
    tables = [slot_table(routes[position]) for position in range(NEW)]
    send_list = []
    for position in range(NEW):
        copies = jnp.repeat(normed[position], TOP, axis=0)
        packed = jnp.dot(
            tables[position].astype(jnp.bfloat16), copies, preferred_element_type=jnp.float32
        )
        packed = packed.astype(jnp.bfloat16).reshape(EXPERTS, CAP, width)
        send_list.append(jnp.repeat(packed, groups, axis=0))
    payload = jnp.concatenate(send_list, axis=1)
    slots = payload.shape[1]
    arrivals = lax.all_to_all(payload, "dp", split_axis=0, concat_axis=0, tiled=True)
    senders, serve_slots, features = arrivals.shape
    partial_value = expert_rows(
        arrivals.reshape(senders * serve_slots, features), w_gate, w_up, w_down
    ).reshape(senders, serve_slots, features)
    back = lax.all_to_all(
        partial_value.astype(jnp.bfloat16), "dp", split_axis=0, concat_axis=0, tiled=True
    ).astype(partial_value.dtype)
    summed_all = jnp.sum(back.reshape(EXPERTS, groups, slots, width), axis=1)
    back_list = [summed_all[:, position * CAP : (position + 1) * CAP] for position in range(NEW)]
    results = []
    for position in range(NEW):
        summed = back_list[position].reshape(EXPERTS * CAP, width)
        per_route = jnp.dot(tables[position].T, summed, preferred_element_type=jnp.float32)
        per_route = per_route.reshape(docs, TOP, width)
        results.append(
            carried[position] + jnp.sum(shares[position][:, :, None] * per_route, axis=1)
        )
    return jnp.stack(results, axis=0).astype(jnp.bfloat16)


def solution(mesh):
    in_specs = (
        P(None, ("grp", "dp"), None),
        P(),
        P(None, ("grp", "dp"), None),
        P(None, ("grp", "dp"), None),
        P(None, ("grp", "dp"), None),
        P(("grp", "dp"), None, None),
        P(("grp", "dp"), None, None),
        P(("grp", "dp")),
        P(None, ("grp", "dp"), None),
        P(None, ("grp", "dp"), None),
        P("dp", None),
        P("dp", None),
        P("dp", None),
    )
    out_specs = P(None, ("grp", "dp"), None)
    return jax.shard_map(
        per_device, mesh=mesh, in_specs=in_specs, out_specs=out_specs, check_vma=False
    )
```

profile of v0, /device:TPU:40, one launch (start us, length us, event | category | flops | bytes accessed | tf_op | source)
XLA Modules:
  0.0 468.3 jit_solution(14173849708833934635)
XLA Ops:
  0.0 0.9 reshape.178
  0.9 1.8 copy.46
  2.8 1.3 bitcast_bitcast_fusion.1
  4.2 2.3 fusion.51
  6.4 0.4 fusion.52
  7.1 0.2 fusion.30
  7.4 0.4 copy.47
  8.0 0.2 fusion.38
  8.2 0.6 copy-done.3
  8.8 0.5 fusion.17
  11.1 2.1 broadcast_in_dim.37
  13.2 2.1 broadcast_in_dim.61
  15.3 4.4 pad_maximum_fusion
  19.7 218.8 %all_to_all.10 = bf16[128,4,4096]{2,1,0:T(4,128)(2,1)} all-to-all(bf16[128,4,4096]{2,1,0:T(4,128)(2,1)S(1)} %pad_maximum_fusion), channel_id=1, replica_groups=mesh['grp'=2,'dp'=128] {'dp'}, dimensions={0} | all-to-all | bytes 8388608 | tf_op jit(solution)/shard_map/all_to_all | solution.py:112
  238.6 6.9 %reshape.189 = bf16[512,4096]{1,0:T(8,128)(2,1)} reshape(bf16[128,4,4096]{2,1,0:T(4,128)(2,1)} %all_to_all.10) | data formatting | bytes 8388608 | tf_op jit(solution)/shard_map/reshape | solution.py:115
  245.5 4.2 fusion.53
  249.7 7.5 %convolution_convert_fusion = bf16[512,4096]{1,0:T(8,128)(2,1)} fusion(bf16[224,4096]{1,0:T(8,128)(2,1)S(1)} %copy-done, bf16[512,4096]{1,0:T(8,128)(2,1)} %reshape.189, bf16[224,4096]{1,0:T(8,128)(2,1)} %param.24, f32[512,224]{0,1:T(8,128)S(1)} %fusion.53), kind=kOutput, calls=%fused_computation.1 | convolution fusion | flops 1881833472 | bytes 12517376 | tf_op jit(solution)/shard_map/dot_general | solution.py:73
  257.2 7.2 %convert_element_type.61 = bf16[128,4,4096]{2,1,0:T(4,128)(2,1)} reshape(bf16[512,4096]{1,0:T(8,128)(2,1)} %convolution_convert_fusion) | data formatting | bytes 8388608 | tf_op jit(solution)/shard_map/convert_element_type | solution.py:118
  264.4 11.4 %all-to-all-start.1 = ((bf16[128,4,4096]{2,1,0:T(4,128)(2,1)}), bf16[128,4,4096]{2,1,0:T(4,128)(2,1)}, u32[]{:S(2)}, u32[]{:S(2)}) async-start(bf16[128,4,4096]{2,1,0:T(4,128)(2,1)} %convert_element_type.61), calls=%async_computation.1 | async-start | bytes 8388608 | tf_op jit(solution)/shard_map/all_to_all | solution.py:117
  276.1 186.5 %all-to-all-done.1 = bf16[128,4,4096]{2,1,0:T(4,128)(2,1)} async-done(((bf16[128,4,4096]{2,1,0:T(4,128)(2,1)}), bf16[128,4,4096]{2,1,0:T(4,128)(2,1)}, u32[]{:S(2)}, u32[]{:S(2)}) %all-to-all-start.1) | async-done | bytes 4194336 | tf_op jit(solution)/shard_map/all_to_all | solution.py:117
  462.6 4.3 convert_reduce_fusion
  467.1 0.2 fusion.21
  467.3 0.3 fusion.20
  467.6 0.7 pad_maximum_fusion.1
  (64 shorter events, 2.8 us)
Async XLA Ops:
  0.0 249.7 %copy-start = (bf16[224,4096]{1,0:T(8,128)(2,1)S(1)}, bf16[224,4096]{1,0:T(8,128)(2,1)}, u32[]{:S(2)}) copy-start(bf16[224,4096]{1,0:T(8,128)(2,1)} %param.25) | copy-start | bytes 5505028
  2.8 1.3 copy-start.10
  2.8 1.4 copy-start.6
  4.1 3.3 copy-start.7
  4.1 3.3 copy-start.1
  6.4 0.7 copy-start.2
  7.8 0.9 copy-start.3
  8.8 0.8 copy-start.4
  8.8 0.9 copy-start.5
  8.8 1.1 copy-start.9
  264.4 11.6 %copy-start.8 = (f32[2,2,2]{2,1,0:T(2,128)S(1)}, f32[2,2,2]{2,1,0:T(2,128)}, u32[]{:S(2)}) copy-start(f32[2,2,2]{2,1,0:T(2,128)} %param.22) | copy-start | bytes 100
  264.4 198.2 %all-to-all-start.1 = ((bf16[128,4,4096]{2,1,0:T(4,128)(2,1)}), bf16[128,4,4096]{2,1,0:T(4,128)(2,1)}, u32[]{:S(2)}, u32[]{:S(2)}) async-start(bf16[128,4,4096]{2,1,0:T(4,128)(2,1)} %convert_element_type.61), calls=%async_computation.1 | async-start | bytes 8388608 | tf_op jit(solution)/shard_map/all_to_all | solution.py:117
where the time goes:
time: 469 us; the launch traced here: 468 us
  blocking collectives  219 us (47%)
  waiting for transfers between devices  186 us (40%)
  local copies, waits for them, and re-layouts  24.5 us (5%)
  matrix products  15.9 us (3%)
  starting transfers between devices  11.4 us (2%)
  other arithmetic  11 us (2%)
    all_to_all x1, blocking collectives, per_device(): lax.all_to_all(payload, 'dp', split_axis=0, concat_axis=0, tiled=True)  219 us
    all_to_all x1, waiting for transfers between devices, per_device(): lax.all_to_all(partial_value.astype(jnp.bfloat16), 'dp', split_axis=0, co...  186 us
    all_to_all x1, starting transfers between devices, per_device(): lax.all_to_all(partial_value.astype(jnp.bfloat16), 'dp', split_axis=0, co...  11.4 us
  transfers between devices with their start and end apart: 1, of which 1 were waited for; matrix products, arithmetic and copies ran while one was open for 0% of the time, Pallas kernels for 0%

commit v1 on v0

--- a/solution.py
+++ b/solution.py
@@ -6,10 +6,9 @@
 HEADS = 32
 KV_HEADS = 8
 HEAD_DIM = 128
-TOP = 2
 EXPERTS = 4
 NEW = 2
-CAP = 2
+RS_TYPE = jnp.bfloat16
 
 
 def attend(queries, new_keys, new_values, cache_keys, cache_values, lengths):
@@ -53,23 +52,14 @@
     return context.reshape(NEW, docs, HEADS * HEAD_DIM)
 
 
-def slot_table(route_rows):
-    flat_ids = route_rows.reshape(-1)
-    matches = (flat_ids[:, None] == jnp.arange(EXPERTS, dtype=jnp.int32)[None, :]).astype(jnp.int32)
-    before = jnp.cumsum(matches, axis=0) - matches
-    slot_ids = flat_ids * CAP + jnp.sum(before * matches, axis=1)
-    slots_all = jnp.arange(EXPERTS * CAP, dtype=jnp.int32)
-    return (slots_all[:, None] == slot_ids[None, :]).astype(jnp.float32)
-
-
-def expert_rows(flat_rows, w_gate, w_up, w_down):
+def expert_rows(flat_rows, row_weight, w_gate, w_up, w_down):
     gate_val = lax.dot_general(
         flat_rows, w_gate, (((1,), (1,)), ((), ())), preferred_element_type=jnp.float32
     )
     up_val = lax.dot_general(
         flat_rows, w_up, (((1,), (1,)), ((), ())), preferred_element_type=jnp.float32
     )
-    act = (jax.nn.silu(gate_val) * up_val).astype(jnp.bfloat16)
+    act = (jax.nn.silu(gate_val) * up_val * row_weight).astype(jnp.bfloat16)
     return jnp.dot(act, w_down, preferred_element_type=jnp.float32)
 
 
@@ -95,39 +85,25 @@
     normed = (
         carried * lax.rsqrt(jnp.mean(carried * carried, -1, keepdims=True) + 1e-05) * norm_gain
     ).astype(jnp.bfloat16)
-    groups = lax.axis_size("dp") // EXPERTS
     top_share = jax.nn.sigmoid(gate_logits[..., 0] - gate_logits[..., 1])
     shares = jnp.stack([top_share, 1.0 - top_share], axis=-1)
-    tables = [slot_table(routes[position]) for position in range(NEW)]
-    send_list = []
-    for position in range(NEW):
-        copies = jnp.repeat(normed[position], TOP, axis=0)
-        packed = jnp.dot(
-            tables[position].astype(jnp.bfloat16), copies, preferred_element_type=jnp.float32
-        )
-        packed = packed.astype(jnp.bfloat16).reshape(EXPERTS, CAP, width)
-        send_list.append(jnp.repeat(packed, groups, axis=0))
-    payload = jnp.concatenate(send_list, axis=1)
-    slots = payload.shape[1]
-    arrivals = lax.all_to_all(payload, "dp", split_axis=0, concat_axis=0, tiled=True)
-    senders, serve_slots, features = arrivals.shape
-    partial_value = expert_rows(
-        arrivals.reshape(senders * serve_slots, features), w_gate, w_up, w_down
-    ).reshape(senders, serve_slots, features)
-    back = lax.all_to_all(
-        partial_value.astype(jnp.bfloat16), "dp", split_axis=0, concat_axis=0, tiled=True
-    ).astype(partial_value.dtype)
-    summed_all = jnp.sum(back.reshape(EXPERTS, groups, slots, width), axis=1)
-    back_list = [summed_all[:, position * CAP : (position + 1) * CAP] for position in range(NEW)]
-    results = []
-    for position in range(NEW):
-        summed = back_list[position].reshape(EXPERTS * CAP, width)
-        per_route = jnp.dot(tables[position].T, summed, preferred_element_type=jnp.float32)
-        per_route = per_route.reshape(docs, TOP, width)
-        results.append(
-            carried[position] + jnp.sum(shares[position][:, :, None] * per_route, axis=1)
-        )
-    return jnp.stack(results, axis=0).astype(jnp.bfloat16)
+    experts = jnp.arange(EXPERTS, dtype=jnp.int32)
+    named = (routes[..., None] == experts).astype(jnp.float32)
+    weights = jnp.sum(shares[..., None] * named, axis=2)
+    rows = NEW * docs
+    devices = lax.axis_size("dp")
+    mine = lax.axis_index("dp") // (devices // EXPERTS)
+    all_rows = lax.all_gather(normed.reshape(rows, width), "dp", axis=0, tiled=True)
+    all_weights = lax.all_gather(weights.reshape(rows, EXPERTS), "dp", axis=0, tiled=True)
+    my_weight = jnp.sum(
+        jnp.where(experts[None, :] == mine, all_weights, 0.0), axis=1, keepdims=True
+    )
+    partial_value = expert_rows(all_rows, my_weight, w_gate, w_up, w_down)
+    summed = lax.psum_scatter(
+        partial_value.astype(RS_TYPE), "dp", scatter_dimension=0, tiled=True
+    )
+    result = carried.reshape(rows, width) + summed.astype(jnp.float32)
+    return result.astype(jnp.bfloat16).reshape(NEW, docs, width)
 
 
 def solution(mesh):

time: 469 us -> 548 us (1.17)
  waiting for transfers between devices: 186 us -> 381 us
  blocking collectives: 219 us -> 120 us
  between operations: 0.31 us -> 14.3 us
  starting transfers between devices: 11.4 us -> 0.07 us
  local copies, waits for them, and re-layouts: 24.5 us -> 15 us
  other arithmetic: 11 us -> 1.92 us
    unnamed x0 -> x3, waiting for transfers between devices: none -> 350 us
    all_to_all x1 -> x0, blocking collectives: 219 us -> none  [per_device(): lax.all_to_all(payload, 'dp', split_axis=0, concat_axis=0, tiled=True)]
    all_to_all x1 -> x0, waiting for transfers between devices: 186 us -> none  [per_device(): lax.all_to_all(partial_value.astype(jnp.bfloat16), 'dp', split_axis=0, co...]
    all_gather x0 -> x1, blocking collectives: none -> 120 us  [per_device(): lax.all_gather(weights.reshape(rows, EXPERTS), 'dp', axis=0, tiled=True)]
    all_gather x0 -> x1, waiting for transfers between devices: none -> 31.2 us  [per_device(): lax.all_gather(normed.reshape(rows, width), 'dp', axis=0, tiled=True)]
    all_to_all x1 -> x0, starting transfers between devices: 11.4 us -> none  [per_device(): lax.all_to_all(partial_value.astype(jnp.bfloat16), 'dp', split_axis=0, co...]
    unnamed x24 -> x29, local copies, waits for them, and re-layouts: 3.21 us -> 11.9 us
    convert_element_type x1 -> x0, local copies, waits for them, and re-layouts: 7.2 us -> none  [per_device(): partial_value.astype(jnp.bfloat16)]
  transfers between devices with their start and end apart: 1 -> 2, of which waited for: 1 -> 2; matrix products, arithmetic and copies ran while one was open for 0% -> 0% of each run, Pallas kernels for 0% -> 0%
where the time goes in v1:
time: 548 us
  waiting for transfers between devices  381 us (70%)
  blocking collectives  120 us (22%)
  matrix products  15.1 us (3%)
  local copies, waits for them, and re-layouts  15 us (3%)
  between operations  14.3 us (3%)
    unnamed x3, waiting for transfers between devices  350 us
    all_gather x1, blocking collectives, per_device(): lax.all_gather(weights.reshape(rows, EXPERTS), 'dp', axis=0, tiled=True)  120 us
    all_gather x1, waiting for transfers between devices, per_device(): lax.all_gather(normed.reshape(rows, width), 'dp', axis=0, tiled=True)  31.2 us
    unnamed x29, local copies, waits for them, and re-layouts  11.9 us
  transfers between devices with their start and end apart: 2, of which 2 were waited for; matrix products, arithmetic and copies ran while one was open for 0% of the time, Pallas kernels for 0%

profile of v1, /device:TPU:40, one launch (start us, length us, event | category | flops | bytes accessed | tf_op | source)
XLA Modules:
  0.0 547.5 jit_solution(5641282166684723363)
XLA Ops:
  6.6 0.9 reshape.89
  7.5 1.8 copy.53
  9.4 1.3 bitcast_bitcast_fusion.1
  10.7 2.3 fusion.41
  13.0 0.4 fusion.42
  13.5 0.1 copy-done.2
  13.7 0.2 fusion.30
  13.9 0.4 copy.54
  14.5 0.2 fusion.36
  14.7 0.6 copy-done.3
  15.3 0.5 fusion.18
  15.9 0.2 copy-done.4
  16.3 0.6 reshape.98
  17.4 120.4 %all-gather.1 = f32[128,4,4]{2,1,0:T(4,128)S(1)} all-gather(f32[1,4,4]{2,1,0:T(4,128)S(1)} %bitcast.39), channel_id=1, replica_groups=mesh['grp'=2,'dp'=128] {'dp'}, dimensions={0}, use_global_device_ids=true | all-gather | bytes 8256 | tf_op jit(solution)/shard_map/all_gather | solution.py:97
  137.8 0.1 select_reduce_fusion
  138.0 31.2 %all-gather.4.cloned.1.call-done = bf16[128,4,4096]{2,1,0:T(4,128)(2,1)} async-done(((bf16[1,4,4096]{2,1,0:T(4,128)(2,1)}), bf16[128,4,4096]{2,1,0:T(4,128)(2,1)}) %all-gather.4.cloned.1.call-update) | async-done | bytes 4194320 | tf_op jit(solution)/shard_map/all_gather | solution.py:96
  169.2 6.9 %reshape.99 = bf16[512,4096]{1,0:T(8,128)(2,1)} reshape(bf16[128,4,4096]{2,1,0:T(4,128)(2,1)} %all-gather.4.cloned.1.call-done) | data formatting | bytes 8388608
  176.1 4.2 fusion.43
  180.3 7.5 %convolution_convert_fusion = bf16[512,4096]{1,0:T(8,128)(2,1)} fusion(bf16[224,4096]{1,0:T(8,128)(2,1)S(1)} %copy-done, bf16[512,4096]{1,0:T(8,128)(2,1)} %reshape.99, bf16[224,4096]{1,0:T(8,128)(2,1)} %param.24, f32[512,224]{0,1:T(8,128)S(1)} %fusion.43, f32[512]{0:T(512)S(1)} %select_reduce_fusion), kind=kOutput, calls=%fused_computation | convolution fusion | flops 1881948160 | bytes 12519424 | tf_op jit(solution)/shard_map/dot_general | solution.py:63
  187.9 0.5 copy-done.11
  188.5 0.6 dynamic-slice
  189.7 349.4 %all-reduce.3.cloned.1.call-done = bf16[512,4096]{1,0:T(8,128)(2,1)} async-done(((bf16[512,4096]{1,0:T(8,128)(2,1)}), bf16[512,4096]{1,0:T(8,128)(2,1)}) %all-reduce.3.cloned.1.call-update) | async-done | bytes 4194320
  539.1 0.9 add_convert_fusion
  540.0 0.6 reshape.97
  (42 shorter events, 1.2 us)
Async XLA Ops:
  6.5 173.8 %copy-start = (bf16[224,4096]{1,0:T(8,128)(2,1)S(1)}, bf16[224,4096]{1,0:T(8,128)(2,1)}, u32[]{:S(2)}) copy-start(bf16[224,4096]{1,0:T(8,128)(2,1)} %param.25) | copy-start | bytes 5505028
  6.6 162.6 %all-gather.4.cloned.1.call-start = ((), (), s32[]{:S(2)}) async-start(), calls=%async_computation | async-start | bytes 4227072 | tf_op jit(solution)/shard_map/all_gather | solution.py:96
  9.3 1.3 copy-start.10
  9.4 1.4 copy-start.6
  10.6 3.3 copy-start.7
  10.6 3.3 copy-start.1
  13.0 0.7 copy-start.2
  14.4 0.9 copy-start.3
  15.3 0.8 copy-start.4
  15.3 0.9 copy-start.5
  15.3 1.8 copy-start.8
  15.3 2.0 copy-start.9
  17.0 522.1 %all-reduce.3.cloned.1.call-start = ((), (), s32[]{:S(2)}) async-start(), calls=%async_computation.1 | async-start | bytes 8388608
  187.8 0.7 copy-start.11
Sparse Core Ops, SparseCore 0:
  17.1 152.0 all-gather.3
  188.0 351.1 all-reduce.2

commit v2 on v1

v2 whole, which is shorter than its diff:
```python
import functools

import jax
import jax.numpy as jnp
from jax import lax
from jax.experimental import pallas as pl
from jax.experimental.pallas import tpu as pltpu
from jax.sharding import PartitionSpec as P

HEADS = 32
KV_HEADS = 8
HEAD_DIM = 128
EXPERTS = 4
NEW = 2
DOC_DEV = 2
ROWS = NEW * DOC_DEV
EXT = 128
TAIL = 128
XS = 4
CORES = 2
MESH = pl.DeviceIdType.MESH
F32 = jnp.float32
BF16 = jnp.bfloat16


def attend_kernel(
    hid_ref, gain_ref, q_ref, nk_ref, nv_ref, ck_ref, cv_ref, len_ref, ext_ref,
    pay_ref, carried_ref, kbuf, vbuf, sems,
):
    docs, cache_len, kv_width = ck_ref.shape
    copies = []
    for d in range(docs):
        for i, (src, dst) in enumerate(((ck_ref, kbuf), (cv_ref, vbuf))):
            copy = pltpu.make_async_copy(
                src.at[d], dst.at[d, pl.ds(0, cache_len)], sems.at[d, i]
            )
            copy.start()
            copies.append(copy)
    q_all = q_ref[...].astype(F32)
    nk_all = nk_ref[...].astype(F32)
    nv_all = nv_ref[...].astype(F32)
    hid_all = hid_ref[...].astype(F32)
    span = cache_len + TAIL
    rows = HEADS * NEW
    per_kv = rows // KV_HEADS
    col = lax.broadcasted_iota(jnp.int32, (rows, span), 1)
    row_at = lax.broadcasted_iota(jnp.int32, (rows, span), 0)
    fresh_ok = (col == cache_len) | ((col == cache_len + 1) & (row_at % NEW == 1))
    block = (
        lax.broadcasted_iota(jnp.int32, (rows, kv_width), 0) // per_kv
        == lax.broadcasted_iota(jnp.int32, (rows, kv_width), 1) // HEAD_DIM
    )
    zeros = jnp.zeros((TAIL - NEW, kv_width), F32)
    parts = []
    for d in range(docs):
        kbuf[d, cache_len:, :] = jnp.concatenate([nk_all[:, d, :], zeros], axis=0).astype(BF16)
        vbuf[d, cache_len:, :] = jnp.concatenate([nv_all[:, d, :], zeros], axis=0).astype(BF16)
        q_doc = q_all[:, d, :]
        q_rows = jnp.concatenate(
            [q_doc[:, h * HEAD_DIM : (h + 1) * HEAD_DIM] for h in range(HEADS)], axis=0
        )
        q_block = jnp.where(block, jnp.concatenate([q_rows] * KV_HEADS, axis=1), 0.0).astype(BF16)
        copies[2 * d].wait()
        scores = lax.dot_general(
            q_block, kbuf[d], (((1,), (1,)), ((), ())), preferred_element_type=F32
        ) * (HEAD_DIM ** (-0.5))
        keep = (col < len_ref[d]) | fresh_ok
        scores = jnp.where(keep, scores, -1e30)
        e = jnp.exp(scores - jnp.max(scores, -1, keepdims=True))
        probs = (e / jnp.sum(e, -1, keepdims=True)).astype(BF16)
        copies[2 * d + 1].wait()
        out = jnp.dot(probs, vbuf[d], preferred_element_type=F32)
        pieces = []
        for h in range(HEADS):
            kv = h * NEW // per_kv
            pieces.append(out[h * NEW : (h + 1) * NEW, kv * HEAD_DIM : (kv + 1) * HEAD_DIM])
        parts.append(hid_all[:, d, :] + jnp.concatenate(pieces, axis=1))
    carried = jnp.concatenate(parts, axis=0)
    carried_ref[...] = carried
    width = carried.shape[1]
    normed = carried * lax.rsqrt(jnp.mean(carried * carried, -1, keepdims=True) + 1e-05)
    pay_ref[:, :width] = (normed * gain_ref[...]).astype(BF16)
    pay_ref[:, width:] = ext_ref[...].astype(BF16)


def attention(hidden_in, norm_gain, queries, new_keys, new_values, cache_keys, cache_values, lengths, ext):
    docs, cache_len, kv_width = cache_keys.shape
    width = hidden_in.shape[2]
    vmem = pl.BlockSpec(memory_space=pltpu.VMEM)
    hbm = pl.BlockSpec(memory_space=pl.ANY)
    return pl.pallas_call(
        attend_kernel,
        name="attend",
        out_shape=(
            jax.ShapeDtypeStruct((ROWS, width + EXT), BF16),
            jax.ShapeDtypeStruct((ROWS, width), F32),
        ),
        in_specs=[vmem, vmem, vmem, vmem, vmem, hbm, hbm, pl.BlockSpec(memory_space=pltpu.SMEM), vmem],
        out_specs=(vmem, vmem),
        scratch_shapes=[
            pltpu.VMEM((docs, cache_len + TAIL, kv_width), BF16),
            pltpu.VMEM((docs, cache_len + TAIL, kv_width), BF16),
            pltpu.SemaphoreType.DMA((docs, 2)),
        ],
    )(hidden_in, norm_gain.reshape(1, width), queries, new_keys, new_values, cache_keys, cache_values, lengths, ext)


def experts_kernel(
    nz, pay_ref, carried_ref, wg_ref, wu_ref, wd_ref, out_ref,
    wg, wu, wd, xin, rows, mine, pair_out, pair_in, ring_out, ring_in, xs_out, xs_in,
    w_sems, xg_send, xg_recv, ag_send, ag_recv, d2_send, d2_recv,
    pr_send, pr_recv, rs_send, rs_recv, xs_send, xs_recv,
):
    me = lax.axis_index("dp")
    core = me % CORES
    x = (me // CORES) % XS
    z = me // (CORES * XS)
    half = nz // 2
    width = carried_ref.shape[1]
    full = width + EXT
    class_rows = XS * ROWS
    slabs_per_expert = nz // EXPERTS
    mine_expert = z // slabs_per_expert

    def at(zz, xx, cc):
        return {"dp": (zz * XS + xx) * CORES + cc}

    def slab_of(offset):
        return lax.rem(z + offset + nz, nz)

    partner = at(z, x, 1 - core)
    step_to = (at(slab_of(1), x, core), at(slab_of(-1), x, core))
    x_peers = [lax.rem(x + k, XS) for k in range(1, XS)]

    w_copies = [
        pltpu.make_async_copy(src, dst, w_sems.at[i])
        for i, (src, dst) in enumerate(((wg_ref, wg), (wu_ref, wu), (wd_ref, wd)))
    ]
    for copy in w_copies:
        copy.start()

    barrier = pltpu.get_barrier_semaphore()
    greeted = [partner, step_to[0], step_to[1]] + [at(z, p, core) for p in x_peers]
    for device in greeted:
        pl.semaphore_signal(barrier, inc=1, device_id=device, device_id_type=MESH)
    pl.semaphore_wait(barrier, len(greeted))

    def remote(src, dst, send, recv, device):
        return pltpu.make_async_remote_copy(
            src_ref=src, dst_ref=dst, send_sem=send, recv_sem=recv,
            device_id=device, device_id_type=MESH,
        )

    xg = [
        remote(pay_ref, xin.at[x], xg_send.at[k], xg_recv.at[k], at(z, p, core))
        for k, p in enumerate(x_peers)
    ]
    for copy in xg:
        copy.start()
    xin[x] = pay_ref[...]
    for copy in xg:
        copy.wait_recv()
    rows[z, 0] = jnp.concatenate([xin[j].astype(F32) for j in range(XS)], axis=0).astype(BF16)

    tiles = full // 128
    cuts = [tiles * i // 4 * 128 for i in range(5)]
    ag_cuts = [pl.ds(cuts[i], cuts[i + 1] - cuts[i]) for i in range(4)]
    sides = ((0, -1), (1, 1))

    def ag_copy(way, sign, s, p):
        ref = rows.at[slab_of(sign * s), 0, :, ag_cuts[p]]
        return remote(ref, ref, ag_send.at[way, s, p], ag_recv.at[way, s, p], step_to[way])

    def d2_copy(way, sign, s):
        slab = slab_of(sign * s)
        return remote(
            rows.at[slab, 0], rows.at[slab, 1], d2_send.at[way, s], d2_recv.at[way, s], partner
        )

    def last_pieces(way):
        return (0, 1) if way == 0 else (2, 3)

    for p in range(4):
        for way, sign in sides:
            ag_copy(way, sign, 0, p).start()
    d2_copy(0, -1, 0).start()

    def gather_step(s, carry):
        for p in range(4):
            for way, sign in sides:
                ag_copy(way, sign, s - 1, p).wait_recv()
                ag_copy(way, sign, s, p).start()
        for way, sign in sides:
            d2_copy(way, sign, s).start()
        return carry

    lax.fori_loop(1, half - 1, gather_step, 0)
    for p in range(4):
        for way, sign in sides:
            ag_copy(way, sign, half - 2, p).wait_recv()
            if p in last_pieces(way):
                ag_copy(way, sign, half - 1, p).start()
    for way, sign in sides:
        d2_copy(way, sign, half - 1).start()
    for way, sign in sides:
        for p in last_pieces(way):
            ag_copy(way, sign, half - 1, p).wait_recv()
    d2_copy(0, -1, half).start()
    for copy in w_copies:
        copy.wait()

    nt = (((1,), (1,)), ((), ()))
    quarter = width // 4

    def expert_rows(offsets, out_way):
        slabs = [slab_of(o) for o in offsets]
        lhs = jnp.concatenate([rows[w, k, :, :width] for w in slabs for k in range(2)], axis=0)
        ext = jnp.concatenate([rows[w, k, :, width:] for w in slabs for k in range(2)], axis=0)
        lane = lax.broadcasted_iota(jnp.int32, ext.shape, 1)
        chosen = (lane == mine_expert) | (lane == mine_expert + EXPERTS)
        weight = jnp.sum(jnp.where(chosen, ext.astype(F32), 0.0), axis=-1, keepdims=True)
        gate = lax.dot_general(lhs, wg[...], nt, preferred_element_type=F32)
        up = lax.dot_general(lhs, wu[...], nt, preferred_element_type=F32)
        act = (jax.nn.silu(gate) * up * weight).astype(BF16)
        for q in range(4):
            cut = slice(q * quarter, (q + 1) * quarter)
            value = jnp.dot(act, wd[:, cut], preferred_element_type=F32)
            for i, w in enumerate(slabs):
                base = 2 * i * class_rows
                mine[w, :, cut] = value[base : base + class_rows]
                pair_out[w, :, cut] = value[base + class_rows : base + 2 * class_rows].astype(BF16)

    def pair_copy(way, offset_abs):
        slab = slab_of(-offset_abs if way == 0 else offset_abs)
        return remote(
            pair_out.at[slab], pair_in.at[slab], pr_send.at[way, offset_abs],
            pr_recv.at[way, offset_abs], partner,
        )

    def d2_wait(way, s):
        d2_copy(way, -1 if way == 0 else 1, s).wait_recv()

    def rs_copy(way, d, p):
        cut = pl.ds(p * quarter, quarter)
        return remote(
            ring_out.at[way, d - 1, :, cut], ring_in.at[way, d - 1, :, cut],
            rs_send.at[way, d - 1, p], rs_recv.at[way, d - 1, p], step_to[way],
        )

    def local_sum(slab, p):
        cut = slice(p * quarter, (p + 1) * quarter)
        return mine[slab, :, cut] + pair_in[slab, :, cut].astype(F32)

    def pass_on(d, has_input):
        for p in range(4):
            for way in range(2):
                cut = slice(p * quarter, (p + 1) * quarter)
                total = local_sum(slab_of(d if way == 0 else -d), p)
                if has_input(way, p):
                    rs_copy(way, d + 1, p).wait_recv()
                    total = total + ring_in[way, d, :, cut].astype(F32)
                ring_out[way, d - 1, :, cut] = total.astype(BF16)
                rs_copy(way, d, p).start()

    d2_wait(1, half - 1)
    d2_wait(0, half - 1)
    d2_wait(0, half)
    expert_rows([half], 0)
    pair_copy(0, half).start()
    expert_rows([half - 1, 1 - half], 0)
    pair_copy(0, half - 1).start()
    pair_copy(1, half - 1).start()
    pair_copy(0, half).wait_recv()
    for way in range(2):
        for p in last_pieces(way):
            cut = slice(p * quarter, (p + 1) * quarter)
            ring_out[way, half - 1, :, cut] = local_sum(slab_of(half), p).astype(BF16)
            rs_copy(way, half, p).start()

    def next_rows(d):
        d2_wait(0, d)
        d2_wait(1, d)
        expert_rows([d, -d], 0)
        pair_copy(0, d).start()
        pair_copy(1, d).start()

    def take_pairs(d):
        pair_copy(0, d).wait_recv()
        pair_copy(1, d).wait_recv()

    next_rows(half - 2)
    take_pairs(half - 1)
    pass_on(half - 1, lambda way, p: p in last_pieces(way))

    def sum_step(i, carry):
        d = half - 2 - i
        next_rows(d - 1)
        take_pairs(d)
        pass_on(d, lambda way, p: True)
        return carry

    lax.fori_loop(0, half - 3, sum_step, 0)
    d2_wait(0, 0)
    expert_rows([0], 0)
    pair_copy(0, 0).start()
    take_pairs(1)
    pass_on(1, lambda way, p: True)

    pair_copy(0, 0).wait_recv()
    for p in range(4):
        cut = slice(p * quarter, (p + 1) * quarter)
        total = local_sum(z, p)
        for way in range(2):
            rs_copy(way, 1, p).wait_recv()
            total = total + ring_in[way, 0, :, cut].astype(F32)
        for j in range(XS):
            xs_out[j, :, cut] = total[j * ROWS : (j + 1) * ROWS].astype(BF16)
    xs = [
        remote(xs_out.at[p], xs_in.at[k], xs_send.at[k], xs_recv.at[k], at(z, p, core))
        for k, p in enumerate(x_peers)
    ]
    for copy in xs:
        copy.start()
    result = carried_ref[...] + xs_out[x].astype(F32)
    for k, copy in enumerate(xs):
        copy.wait_recv()
        result = result + xs_in[k].astype(F32)
    for d in range(DOC_DEV):
        for t in range(NEW):
            r = d * NEW + t
            out_ref[t, d : d + 1, :] = result[r : r + 1].astype(BF16)

    for copy in xg + xs:
        copy.wait_send()

    def drain(s, carry):
        for p in range(4):
            for way, sign in sides:
                ag_copy(way, sign, s, p).wait_send()
                rs_copy(way, s + 1, p).wait_send()
        for way, sign in sides:
            d2_copy(way, sign, s + 1).wait_send()
            pair_copy(way, s + 1).wait_send()
        return carry

    lax.fori_loop(0, half - 1, drain, 0)
    for way, sign in sides:
        for p in last_pieces(way):
            ag_copy(way, sign, half - 1, p).wait_send()
            rs_copy(way, half, p).wait_send()
    for s in (0, half):
        d2_copy(0, -1, s).wait_send()
        pair_copy(0, s).wait_send()


def experts(payload, carried, w_gate, w_up, w_down, nz):
    width = carried.shape[1]
    hidden = w_gate.shape[0]
    half = nz // 2
    class_rows = XS * ROWS
    vmem = pl.BlockSpec(memory_space=pltpu.VMEM)
    hbm = pl.BlockSpec(memory_space=pl.ANY)
    dma = pltpu.SemaphoreType.DMA
    return pl.pallas_call(
        functools.partial(experts_kernel, nz),
        name="experts",
        out_shape=jax.ShapeDtypeStruct((NEW, DOC_DEV, width), BF16),
        in_specs=[vmem, vmem, hbm, hbm, hbm],
        out_specs=vmem,
        scratch_shapes=[
            pltpu.VMEM((hidden, width), BF16),
            pltpu.VMEM((hidden, width), BF16),
            pltpu.VMEM((hidden, width), BF16),
            pltpu.VMEM((XS, ROWS, width + EXT), BF16),
            pltpu.VMEM((nz, 2, class_rows, width + EXT), BF16),
            pltpu.VMEM((nz, class_rows, width), F32),
            pltpu.VMEM((nz, class_rows, width), BF16),
            pltpu.VMEM((nz, class_rows, width), BF16),
            pltpu.VMEM((2, half, class_rows, width), BF16),
            pltpu.VMEM((2, half, class_rows, width), BF16),
            pltpu.VMEM((XS, ROWS, width), BF16),
            pltpu.VMEM((XS - 1, ROWS, width), BF16),
            dma((3,)),
            dma((XS - 1,)), dma((XS - 1,)),
            dma((2, half, 4)), dma((2, half, 4)),
            dma((2, half + 1)), dma((2, half + 1)),
            dma((2, half + 1)), dma((2, half + 1)),
            dma((2, half, 4)), dma((2, half, 4)),
            dma((XS - 1,)), dma((XS - 1,)),
        ],
        compiler_params=pltpu.CompilerParams(
            collective_id=0, has_side_effects=True, vmem_limit_bytes=56 * 1024 * 1024
        ),
    )(payload, carried, w_gate, w_up, w_down)


def per_device(
    hidden_in, norm_gain, queries, new_keys, new_values, cache_keys, cache_values,
    lengths, routes, gate_logits, w_gate, w_up, w_down,
):
    top_share = jax.nn.sigmoid(gate_logits[..., 0] - gate_logits[..., 1])
    shares = jnp.stack([top_share, 1.0 - top_share], axis=-1)
    lanes = jnp.arange(EXT, dtype=jnp.int32)
    weights = jnp.sum(shares[..., None] * (routes[..., None] == lanes % EXPERTS), axis=2)
    weights = jnp.swapaxes(weights, 0, 1).reshape(ROWS, EXT)
    high = lax.reduce_precision(weights, 8, 7)
    ext = jnp.where(lanes < EXPERTS, high, jnp.where(lanes < 2 * EXPERTS, weights - high, 0.0))
    payload, carried = attention(
        hidden_in, norm_gain, queries, new_keys, new_values, cache_keys, cache_values, lengths, ext
    )
    nz = lax.axis_size("dp") // (XS * CORES)
    return experts(payload, carried, w_gate, w_up, w_down, nz)


def solution(mesh):
    in_specs = (
        P(None, ("grp", "dp"), None),
        P(),
        P(None, ("grp", "dp"), None),
        P(None, ("grp", "dp"), None),
        P(None, ("grp", "dp"), None),
        P(("grp", "dp"), None, None),
        P(("grp", "dp"), None, None),
        P(("grp", "dp")),
        P(None, ("grp", "dp"), None),
        P(None, ("grp", "dp"), None),
        P("dp", None),
        P("dp", None),
        P("dp", None),
    )
    out_specs = P(None, ("grp", "dp"), None)
    return jax.shard_map(
        per_device, mesh=mesh, in_specs=in_specs, out_specs=out_specs, check_vma=False
    )
```

time: 548 us -> 109 us (0.20)
  waiting for transfers between devices: 381 us -> 0 us
  blocking collectives: 120 us -> 0 us
  Pallas kernels: 0 us -> 105 us
  matrix products: 15.1 us -> 0 us
  between operations: 14.3 us -> 0.02 us
  local copies, waits for them, and re-layouts: 15 us -> 1.4 us
    unnamed x3 -> x0, waiting for transfers between devices: 350 us -> none
    all_gather x1 -> x0, blocking collectives: 120 us -> none  [per_device(): lax.all_gather(weights.reshape(rows, EXPERTS), 'dp', axis=0, tiled=True)]
    pallas_call x0 -> x2, Pallas kernels: none -> 105 us  [the longest x1 100 us: experts(): pl.pallas_call(functools.partial(experts_kernel, nz), name='experts', out...]
    all_gather x1 -> x0, waiting for transfers between devices: 31.2 us -> none  [per_device(): lax.all_gather(normed.reshape(rows, width), 'dp', axis=0, tiled=True)]
    dot_general x6 -> x0, matrix products: 15.1 us -> none  [the longest x1 7.49 us: expert_rows(): return jnp.dot(act, w_down, preferred_element_type=jnp.float32)]
    unnamed x29 -> x1, local copies, waits for them, and re-layouts: 11.9 us -> 1.4 us
  transfers between devices with their start and end apart: 2 -> 0, of which waited for: 2 -> 0; matrix products, arithmetic and copies ran while one was open for 0% -> 0% of each run, Pallas kernels for 0% -> 0%
where the time goes in v2:
time: 109 us
  Pallas kernels  105 us (96%)
  other arithmetic  2.29 us (2%)
  local copies, waits for them, and re-layouts  1.4 us (1%)
    pallas_call x1, Pallas kernels, experts(): pl.pallas_call(functools.partial(experts_kernel, nz), name='experts', out...  100 us
    pallas_call x1, Pallas kernels, attention(): pl.pallas_call(attend_kernel, name='attend', out_shape=(jax.ShapeDtypeStr...  4.59 us

profile of v2, /device:TPU:40, one launch (start us, length us, event | category | flops | bytes accessed | tf_op | source)
XLA Modules:
  0.0 108.7 jit_solution(12165159548945698167)
XLA Ops:
  0.0 0.8 broadcast_subtract_fusion
  0.9 0.1 pad_maximum_fusion
  0.9 0.8 fusion
  1.7 0.6 reduce-precision_select_fusion.ext_ref
  2.3 4.6 %attend.1 = (bf16[4,4224]{1,0:T(4,128)(2,1)}, f32[4,4096]{1,0:T(4,128)}) custom-call(bf16[2,2,4096]{2,1,0:T(2,128)(2,1)} %hid_ref.1, f32[1,4096]{1,0:T(1,128)} %bitcast.3, bf16[2,2,4096]{2,1,0:T(2,128)(2,1)} %q_ref.1, bf16[2,2,1024]{2,1,0:T(2,128)(2,1)} %nk_ref.1, bf16[2,2,1024]{2,1,0:T(2,128)(2,1)} %nv_ref.1, bf16[2,384,1024]{2,1,0:T(8,128)(2,1)} %ck_ref.1, ...), custom_call_target="tpu_custom_call" | custom-call | tf_op jit(solution)/shard_map/attend/pallas_call | solution.py:91
  6.9 100.4 %experts.1 = bf16[2,2,4096]{2,1,0:T(2,128)(2,1)} custom-call(bf16[4,4224]{1,0:T(4,128)(2,1)} %get-tuple-element.7.pay_ref, f32[4,4096]{1,0:T(4,128)} %get-tuple-element.8.carried_ref, bf16[224,4096]{1,0:T(8,128)(2,1)} %wg_ref.1, bf16[224,4096]{1,0:T(8,128)(2,1)} %wu_ref.1, bf16[224,4096]{1,0:T(8,128)(2,1)} %wd_ref.1), custom_call_target="tpu_custom_call" | custom-call | tf_op jit(solution)/shard_map/experts/pallas_call | solution.py:364
  107.3 1.4 %copy.16 = bf16[2,2,4096]{2,1,0:T(2,128)(2,1)} copy(bf16[2,2,4096]{2,1,0:T(2,128)(2,1)} %experts.1) | data formatting | bytes 65536
  (3 shorter events, 0.0 us)

commit v3 on v1

v3 whole, which is shorter than its diff:
```python
import functools

import jax
import jax.numpy as jnp
from jax import lax
from jax.experimental import pallas as pl
from jax.experimental.pallas import tpu as pltpu
from jax.sharding import PartitionSpec as P

HEADS = 32
KV_HEADS = 8
HEAD_DIM = 128
EXPERTS = 4
NEW = 2
DOC_DEV = 2
ROWS = NEW * DOC_DEV
EXT = 128
TAIL = 128
XS = 4
PIECES = 4
CORES = 2
MESH = pl.DeviceIdType.MESH
F32 = jnp.float32
BF16 = jnp.bfloat16


def layer_kernel(
    nz, hid_hbm, gain_hbm, q_hbm, nk_hbm, nv_hbm, ck_hbm, cv_hbm, len_ref, routes_ref, logits_ref,
    wg_hbm, wu_hbm, wd_hbm, out_ref,
    hid, gain, q, nk, nv, kbuf, vbuf, wg, wu, wd, carried_ref,
    xin, rows, mine, pair_out, pair_in, ring_out, ring_in, xs_out, xs_in,
    in_sems, kv_sems, w_sems, xg_send, xg_recv, ag_send, ag_recv, d2_send, d2_recv,
    pr_send, pr_recv, rs_send, rs_recv, xs_send, xs_recv,
):
    me = lax.axis_index("dp")
    core = me % CORES
    x = (me // CORES) % XS
    z = me // (CORES * XS)
    half = nz // 2
    width = carried_ref.shape[1]
    full = width + EXT
    class_rows = XS * ROWS
    mine_expert = z // (nz // EXPERTS)
    docs, span, kv_width = kbuf.shape
    cache_len = span - TAIL

    def at(zz, xx, cc):
        return {"dp": (zz * XS + xx) * CORES + cc}

    def slab_of(offset):
        return lax.rem(z + offset + nz, nz)

    partner = at(z, x, 1 - core)
    step_to = (at(slab_of(1), x, core), at(slab_of(-1), x, core))
    x_peers = [lax.rem(x + k, XS) for k in range(1, XS)]

    barrier = pltpu.get_barrier_semaphore()
    greeted = [partner, step_to[0], step_to[1]] + [at(z, p, core) for p in x_peers]
    for device in greeted:
        pl.semaphore_signal(barrier, inc=1, device_id=device, device_id_type=MESH)

    small = [
        pltpu.make_async_copy(src, dst, in_sems.at[i])
        for i, (src, dst) in enumerate(
            ((q_hbm, q), (nk_hbm, nk), (nv_hbm, nv), (hid_hbm, hid), (gain_hbm, gain))
        )
    ]
    kv = [
        pltpu.make_async_copy(src.at[d], dst.at[d, pl.ds(0, cache_len)], kv_sems.at[d, i])
        for d in range(docs)
        for i, (src, dst) in enumerate(((ck_hbm, kbuf), (cv_hbm, vbuf)))
    ]
    w_copies = [
        pltpu.make_async_copy(src, dst, w_sems.at[i])
        for i, (src, dst) in enumerate(((wg_hbm, wg), (wu_hbm, wu), (wd_hbm, wd)))
    ]
    for copy in small[:3] + kv + small[3:] + w_copies:
        copy.start()

    heads_rows = HEADS * NEW
    per_kv = heads_rows // KV_HEADS
    col = lax.broadcasted_iota(jnp.int32, (heads_rows, span), 1)
    row_at = lax.broadcasted_iota(jnp.int32, (heads_rows, span), 0)
    fresh_ok = (col == cache_len) | ((col == cache_len + 1) & (row_at % NEW == 1))
    block = (
        lax.broadcasted_iota(jnp.int32, (heads_rows, kv_width), 0) // per_kv
        == lax.broadcasted_iota(jnp.int32, (heads_rows, kv_width), 1) // HEAD_DIM
    )
    zeros = jnp.zeros((TAIL - NEW, kv_width), F32)

    lane = lax.broadcasted_iota(jnp.int32, (ROWS, EXT), 1)
    at_row = lax.broadcasted_iota(jnp.int32, (ROWS, EXT), 0)

    def by_row(values):
        out = jnp.full((ROWS, EXT), values[0])
        for r in range(1, ROWS):
            out = jnp.where(at_row == r, values[r], out)
        return out

    order = [(t, d) for d in range(DOC_DEV) for t in range(NEW)]
    first = by_row([routes_ref[t, d, 0] for t, d in order])
    second = by_row([routes_ref[t, d, 1] for t, d in order])
    share = jax.nn.sigmoid(by_row([logits_ref[t, d, 0] - logits_ref[t, d, 1] for t, d in order]))
    expert_at = lane % EXPERTS
    weights = jnp.where(expert_at == first, share, 0.0) + jnp.where(
        expert_at == second, 1.0 - share, 0.0
    )
    high = weights.astype(BF16)
    low = (weights - high.astype(F32)).astype(BF16)
    zero_ext = jnp.zeros_like(high)
    ext = jnp.where(lane < EXPERTS, high, jnp.where(lane < 2 * EXPERTS, low, zero_ext))

    for copy in small[:3]:
        copy.wait()
    q_all = q[...].astype(F32)
    nk_all = nk[...].astype(F32)
    nv_all = nv[...].astype(F32)
    q_blocks = []
    for d in range(docs):
        kbuf[d, cache_len:, :] = jnp.concatenate([nk_all[:, d, :], zeros], axis=0).astype(BF16)
        vbuf[d, cache_len:, :] = jnp.concatenate([nv_all[:, d, :], zeros], axis=0).astype(BF16)
        q_doc = q_all[:, d, :]
        q_rows = jnp.concatenate(
            [q_doc[:, h * HEAD_DIM : (h + 1) * HEAD_DIM] for h in range(HEADS)], axis=0
        )
        q_blocks.append(
            jnp.where(block, jnp.concatenate([q_rows] * KV_HEADS, axis=1), 0.0).astype(BF16)
        )
    parts = []
    for d in range(docs):
        kv[2 * d].wait()
        scores = lax.dot_general(
            q_blocks[d], kbuf[d], (((1,), (1,)), ((), ())), preferred_element_type=F32
        ) * (HEAD_DIM ** (-0.5))
        keep = (col < len_ref[d]) | fresh_ok
        scores = jnp.where(keep, scores, -1e30)
        e = jnp.exp(scores - jnp.max(scores, -1, keepdims=True))
        probs = (e / jnp.sum(e, -1, keepdims=True)).astype(BF16)
        kv[2 * d + 1].wait()
        out = jnp.dot(probs, vbuf[d], preferred_element_type=F32)
        pieces = []
        for h in range(HEADS):
            k = h * NEW // per_kv
            pieces.append(out[h * NEW : (h + 1) * NEW, k * HEAD_DIM : (k + 1) * HEAD_DIM])
        parts.append(jnp.concatenate(pieces, axis=1))
    for copy in small[3:]:
        copy.wait()
    hid_all = hid[...].astype(F32)
    carried = jnp.concatenate([hid_all[:, d, :] + parts[d] for d in range(docs)], axis=0)
    carried_ref[...] = carried
    normed = carried * lax.rsqrt(jnp.mean(carried * carried, -1, keepdims=True) + 1e-05)
    xin[x, :, :width] = (normed * gain[...]).astype(BF16)
    xin[x, :, width:] = ext
    pl.semaphore_wait(barrier, len(greeted))

    def remote(src, dst, send, recv, device):
        return pltpu.make_async_remote_copy(
            src_ref=src, dst_ref=dst, send_sem=send, recv_sem=recv,
            device_id=device, device_id_type=MESH,
        )

    def whole(ref, send, recv):
        return remote(ref, ref, send, recv, partner)

    for p in x_peers:
        remote(xin.at[x], xin.at[x], xg_send.at[0], xg_recv.at[0], at(z, p, core)).start()
    xg_all = whole(xin.at[pl.ds(0, XS - 1)], xg_send.at[0], xg_recv.at[0])
    xg_all.wait_recv()
    rows[z, 0] = jnp.concatenate([xin[j].astype(F32) for j in range(XS)], axis=0).astype(BF16)

    tiles = full // 128
    cuts = [tiles * i // PIECES * 128 for i in range(PIECES + 1)]
    ag_cuts = [pl.ds(cuts[i], cuts[i + 1] - cuts[i]) for i in range(PIECES)]
    sides = ((0, -1), (1, 1))

    def ag_copy(way, sign, s, p, last=0):
        ref = rows.at[slab_of(sign * s), 0, :, ag_cuts[p]]
        return remote(ref, ref, ag_send.at[way, last], ag_recv.at[way, s, p], step_to[way])

    def d2_copy(way, sign, s):
        slab = slab_of(sign * s)
        return remote(rows.at[slab, 0], rows.at[slab, 1], d2_send.at[0], d2_recv.at[s], partner)

    def d2_wait(s, count):
        whole(rows.at[pl.ds(0, count), 1], d2_send.at[0], d2_recv.at[s]).wait_recv()

    def last_pieces(way):
        return tuple(range(PIECES // 2)) if way == 0 else tuple(range(PIECES // 2, PIECES))

    for p in range(PIECES):
        for way, sign in sides:
            ag_copy(way, sign, 0, p).start()
    d2_copy(0, -1, 0).start()

    def gather_step(s, carry):
        for p in range(PIECES):
            for way, sign in sides:
                ag_copy(way, sign, s - 1, p).wait_recv()
                ag_copy(way, sign, s, p).start()
        for way, sign in sides:
            d2_copy(way, sign, s).start()
        return carry

    nt = (((1,), (1,)), ((), ()))
    quarter = width // 4
    piece = width // PIECES

    def expert_rows(offsets):
        slabs = [slab_of(o) for o in offsets]
        lhs = jnp.concatenate([rows[w, k, :, :width] for w in slabs for k in range(2)], axis=0)
        tail = jnp.concatenate([rows[w, k, :, width:] for w in slabs for k in range(2)], axis=0)
        lanes = lax.broadcasted_iota(jnp.int32, tail.shape, 1)
        chosen = (lanes == mine_expert) | (lanes == mine_expert + EXPERTS)
        weight = jnp.sum(jnp.where(chosen, tail.astype(F32), 0.0), axis=-1, keepdims=True)
        gate = lax.dot_general(lhs, wg[...], nt, preferred_element_type=F32)
        up = lax.dot_general(lhs, wu[...], nt, preferred_element_type=F32)
        act = (jax.nn.silu(gate) * up * weight).astype(BF16)
        for c in range(4):
            cut = slice(c * quarter, (c + 1) * quarter)
            value = jnp.dot(act, wd[:, cut], preferred_element_type=F32)
            for i, w in enumerate(slabs):
                base = 2 * i * class_rows
                mine[w, :, cut] = value[base : base + class_rows]
                pair_out[w, :, cut] = value[base + class_rows : base + 2 * class_rows].astype(BF16)

    def pair_copy(way, d):
        slab = slab_of(-d if way == 0 else d)
        return remote(
            pair_out.at[slab], pair_in.at[slab], pr_send.at[0], pr_recv.at[d], partner
        )

    def pair_wait(d, count):
        whole(pair_in.at[pl.ds(0, count)], pr_send.at[0], pr_recv.at[d]).wait_recv()

    def next_rows(d):
        d2_wait(d, 2)
        expert_rows([d, -d])
        pair_copy(0, d).start()
        pair_copy(1, d).start()

    lax.fori_loop(1, half - 1, gather_step, 0)
    for p in range(PIECES):
        for way, sign in sides:
            ag_copy(way, sign, half - 2, p).wait_recv()
            if p in last_pieces(way):
                ag_copy(way, sign, half - 1, p, 1).start()
    for way, sign in sides:
        d2_copy(way, sign, half - 1).start()
    for copy in w_copies:
        copy.wait()
    next_rows(half - 2)
    for way, sign in sides:
        for p in last_pieces(way):
            ag_copy(way, sign, half - 1, p).wait_recv()
    d2_copy(0, -1, half).start()
    next_rows(half - 1)
    d2_wait(half, 1)
    expert_rows([half])
    pair_copy(0, half).start()

    def rs_copy(way, d, p, last=0):
        cut = pl.ds(p * piece, piece)
        return remote(
            ring_out.at[way, d - 1, :, cut], ring_in.at[way, d - 1, :, cut],
            rs_send.at[way, last], rs_recv.at[way, d - 1, p], step_to[way],
        )

    def local_sum(slab, p):
        cut = slice(p * piece, (p + 1) * piece)
        return mine[slab, :, cut] + pair_in[slab, :, cut].astype(F32)

    def pass_on(d, has_input):
        for p in range(PIECES):
            for way in range(2):
                cut = slice(p * piece, (p + 1) * piece)
                total = local_sum(slab_of(d if way == 0 else -d), p)
                if has_input(way, p):
                    rs_copy(way, d + 1, p).wait_recv()
                    total = total + ring_in[way, d, :, cut].astype(F32)
                ring_out[way, d - 1, :, cut] = total.astype(BF16)
                rs_copy(way, d, p).start()

    pair_wait(half, 1)
    for way in range(2):
        for p in last_pieces(way):
            cut = slice(p * piece, (p + 1) * piece)
            ring_out[way, half - 1, :, cut] = local_sum(slab_of(half), p).astype(BF16)
            rs_copy(way, half, p, 1).start()
    pair_wait(half - 1, 2)
    next_rows(half - 3)
    pass_on(half - 1, lambda way, p: p in last_pieces(way))

    def sum_step(i, carry):
        d = half - 2 - i
        next_rows(d - 2)
        pair_wait(d, 2)
        pass_on(d, lambda way, p: True)
        return carry

    lax.fori_loop(0, half - 4, sum_step, 0)
    d2_wait(0, 1)
    expert_rows([0])
    pair_copy(0, 0).start()
    for d in (2, 1):
        pair_wait(d, 2)
        pass_on(d, lambda way, p: True)

    pair_wait(0, 1)
    for p in range(PIECES):
        cut = slice(p * piece, (p + 1) * piece)
        total = local_sum(z, p)
        for way in range(2):
            rs_copy(way, 1, p).wait_recv()
            total = total + ring_in[way, 0, :, cut].astype(F32)
        for j in range(XS):
            xs_out[j, :, cut] = total[j * ROWS : (j + 1) * ROWS].astype(BF16)
    for k, p in enumerate(x_peers):
        remote(xs_out.at[p], xs_in.at[k], xs_send.at[0], xs_recv.at[0], at(z, p, core)).start()
    result = carried_ref[...] + xs_out[x].astype(F32)
    xs_all = whole(xs_in, xs_send.at[0], xs_recv.at[0])
    xs_all.wait_recv()
    for k in range(XS - 1):
        result = result + xs_in[k].astype(F32)
    for d in range(DOC_DEV):
        for t in range(NEW):
            r = d * NEW + t
            out_ref[t, d : d + 1, :] = result[r : r + 1].astype(BF16)

    xg_all.wait_send()
    xs_all.wait_send()
    for way in range(2):
        part = pl.ds(cuts[last_pieces(way)[0]], cuts[last_pieces(way)[-1] + 1] - cuts[last_pieces(way)[0]])
        whole(rows.at[pl.ds(0, half - 1), 0], ag_send.at[way, 0], ag_recv.at[0, 0, 0]).wait_send()
        whole(rows.at[0, 0, :, part], ag_send.at[way, 1], ag_recv.at[0, 0, 0]).wait_send()
        whole(ring_out.at[0, pl.ds(0, half - 1)], rs_send.at[way, 0], rs_recv.at[0, 0, 0]).wait_send()
        whole(
            ring_out.at[0, 0, :, pl.ds(0, width // 2)], rs_send.at[way, 1], rs_recv.at[0, 0, 0]
        ).wait_send()
    whole(rows.at[:, 0], d2_send.at[0], d2_recv.at[0]).wait_send()
    whole(pair_out, pr_send.at[0], pr_recv.at[0]).wait_send()


def per_device(
    hidden_in, norm_gain, queries, new_keys, new_values, cache_keys, cache_values,
    lengths, routes, gate_logits, w_gate, w_up, w_down,
):
    nz = lax.axis_size("dp") // (XS * CORES)
    half = nz // 2
    width = hidden_in.shape[2]
    docs, cache_len, kv_width = cache_keys.shape
    hidden = w_gate.shape[0]
    full = width + EXT
    class_rows = XS * ROWS
    vmem = pl.BlockSpec(memory_space=pltpu.VMEM)
    smem = pl.BlockSpec(memory_space=pltpu.SMEM)
    hbm = pl.BlockSpec(memory_space=pl.ANY)
    dma = pltpu.SemaphoreType.DMA
    return pl.pallas_call(
        functools.partial(layer_kernel, nz),
        name="layer",
        out_shape=jax.ShapeDtypeStruct(hidden_in.shape, BF16),
        in_specs=[hbm] * 7 + [smem] * 3 + [hbm] * 3,
        out_specs=vmem,
        scratch_shapes=[
            pltpu.VMEM(hidden_in.shape, BF16),
            pltpu.VMEM((1, width), F32),
            pltpu.VMEM(queries.shape, BF16),
            pltpu.VMEM(new_keys.shape, BF16),
            pltpu.VMEM(new_values.shape, BF16),
            pltpu.VMEM((docs, cache_len + TAIL, kv_width), BF16),
            pltpu.VMEM((docs, cache_len + TAIL, kv_width), BF16),
            pltpu.VMEM((hidden, width), BF16),
            pltpu.VMEM((hidden, width), BF16),
            pltpu.VMEM((hidden, width), BF16),
            pltpu.VMEM((ROWS, width), F32),
            pltpu.VMEM((XS, ROWS, full), BF16),
            pltpu.VMEM((nz, 2, class_rows, full), BF16),
            pltpu.VMEM((nz, class_rows, width), F32),
            pltpu.VMEM((nz, class_rows, width), BF16),
            pltpu.VMEM((nz, class_rows, width), BF16),
            pltpu.VMEM((2, half, class_rows, width), BF16),
            pltpu.VMEM((2, half, class_rows, width), BF16),
            pltpu.VMEM((XS, ROWS, width), BF16),
            pltpu.VMEM((XS - 1, ROWS, width), BF16),
            dma((5,)), dma((docs, 2)), dma((3,)),
            dma((1,)), dma((1,)),
            dma((2, 2)), dma((2, half, PIECES)),
            dma((1,)), dma((half + 1,)),
            dma((1,)), dma((half + 1,)),
            dma((2, 2)), dma((2, half, PIECES)),
            dma((1,)), dma((1,)),
        ],
        compiler_params=pltpu.CompilerParams(
            collective_id=0, has_side_effects=True, vmem_limit_bytes=56 * 1024 * 1024
        ),
    )(
        hidden_in, norm_gain.reshape(1, width), queries, new_keys, new_values, cache_keys,
        cache_values, lengths, routes, gate_logits, w_gate, w_up, w_down,
    )


def solution(mesh):
    in_specs = (
        P(None, ("grp", "dp"), None),
        P(),
        P(None, ("grp", "dp"), None),
        P(None, ("grp", "dp"), None),
        P(None, ("grp", "dp"), None),
        P(("grp", "dp"), None, None),
        P(("grp", "dp"), None, None),
        P(("grp", "dp")),
        P(None, ("grp", "dp"), None),
        P(None, ("grp", "dp"), None),
        P("dp", None),
        P("dp", None),
        P("dp", None),
    )
    out_specs = P(None, ("grp", "dp"), None)
    return jax.shard_map(
        per_device, mesh=mesh, in_specs=in_specs, out_specs=out_specs, check_vma=False
    )
```

time: 548 us -> 102 us (0.19)
  waiting for transfers between devices: 381 us -> 0 us
  blocking collectives: 120 us -> 0 us
  Pallas kernels: 0 us -> 100 us
  matrix products: 15.1 us -> 0 us
  between operations: 14.3 us -> 0.01 us
  local copies, waits for them, and re-layouts: 15 us -> 1.4 us
    unnamed x3 -> x0, waiting for transfers between devices: 350 us -> none
    all_gather x1 -> x0, blocking collectives: 120 us -> none  [per_device(): lax.all_gather(weights.reshape(rows, EXPERTS), 'dp', axis=0, tiled=True)]
    pallas_call x0 -> x1, Pallas kernels: none -> 100 us  [per_device(): pl.pallas_call(functools.partial(layer_kernel, nz), name='layer', out_sha...]
    all_gather x1 -> x0, waiting for transfers between devices: 31.2 us -> none  [per_device(): lax.all_gather(normed.reshape(rows, width), 'dp', axis=0, tiled=True)]
    dot_general x6 -> x0, matrix products: 15.1 us -> none  [the longest x1 7.49 us: expert_rows(): return jnp.dot(act, w_down, preferred_element_type=jnp.float32)]
    unnamed x29 -> x1, local copies, waits for them, and re-layouts: 11.9 us -> 1.4 us
  transfers between devices with their start and end apart: 2 -> 0, of which waited for: 2 -> 0; matrix products, arithmetic and copies ran while one was open for 0% -> 0% of each run, Pallas kernels for 0% -> 0%
where the time goes in v3:
time: 102 us; the launch traced here: 101 us
  Pallas kernels  100 us (98%)
  local copies, waits for them, and re-layouts  1.4 us (1%)
    pallas_call x1, Pallas kernels, per_device(): pl.pallas_call(functools.partial(layer_kernel, nz), name='layer', out_sha...  100 us

profile of v3, /device:TPU:40, one launch (start us, length us, event | category | flops | bytes accessed | tf_op | source)
XLA Modules:
  0.0 101.5 jit_solution(11595040542348481497)
XLA Ops:
  0.0 100.1 %layer.1 = bf16[2,2,4096]{2,1,0:T(2,128)(2,1)} custom-call(bf16[2,2,4096]{2,1,0:T(2,128)(2,1)} %hid_hbm.1, f32[1,4096]{1,0:T(1,128)} %bitcast.1, bf16[2,2,4096]{2,1,0:T(2,128)(2,1)} %q_hbm.1, bf16[2,2,1024]{2,1,0:T(2,128)(2,1)} %nk_hbm.1, bf16[2,2,1024]{2,1,0:T(2,128)(2,1)} %nv_hbm.1, bf16[2,384,1024]{2,1,0:T(8,128)(2,1)} %ck_hbm.1, ...), custom_call_target="tpu_custom_call" | custom-call | tf_op jit(solution)/shard_map/layer/pallas_call | solution.py:358
  100.1 1.4 %copy.15 = bf16[2,2,4096]{2,1,0:T(2,128)(2,1)} copy(bf16[2,2,4096]{2,1,0:T(2,128)(2,1)} %layer.1) | data formatting | bytes 65536

commit v4 on v3

--- a/solution.py
+++ b/solution.py
@@ -17,6 +17,7 @@
 EXT = 128
 TAIL = 128
 XS = 4
+RADIUS = 2
 PIECES = 4
 CORES = 2
 MESH = pl.DeviceIdType.MESH
@@ -28,8 +29,8 @@
     nz, hid_hbm, gain_hbm, q_hbm, nk_hbm, nv_hbm, ck_hbm, cv_hbm, len_ref, routes_ref, logits_ref,
     wg_hbm, wu_hbm, wd_hbm, out_ref,
     hid, gain, q, nk, nv, kbuf, vbuf, wg, wu, wd, carried_ref,
-    xin, rows, mine, pair_out, pair_in, ring_out, ring_in, xs_out, xs_in,
-    in_sems, kv_sems, w_sems, xg_send, xg_recv, ag_send, ag_recv, d2_send, d2_recv,
+    cols, rows, mine, pair_out, pair_in, ring_out, ring_in, xs_out, xs_in,
+    in_sems, kv_sems, w_sems, zg_send, zg_recv, xf_send, xf_recv, xr_send, xr_recv, d2_send, d2_recv,
     pr_send, pr_recv, rs_send, rs_recv, xs_send, xs_recv,
 ):
     me = lax.axis_index("dp")
@@ -55,7 +56,9 @@
     x_peers = [lax.rem(x + k, XS) for k in range(1, XS)]
 
     barrier = pltpu.get_barrier_semaphore()
-    greeted = [partner, step_to[0], step_to[1]] + [at(z, p, core) for p in x_peers]
+    greeted = [partner] + [at(z, p, core) for p in x_peers]
+    for r in range(1, RADIUS + 1):
+        greeted += [at(slab_of(r), x, core), at(slab_of(-r), x, core)]
     for device in greeted:
         pl.semaphore_signal(barrier, inc=1, device_id=device, device_id_type=MESH)
 
@@ -149,8 +152,8 @@
     carried = jnp.concatenate([hid_all[:, d, :] + parts[d] for d in range(docs)], axis=0)
     carried_ref[...] = carried
     normed = carried * lax.rsqrt(jnp.mean(carried * carried, -1, keepdims=True) + 1e-05)
-    xin[x, :, :width] = (normed * gain[...]).astype(BF16)
-    xin[x, :, width:] = ext
+    cols[z, x, :, :width] = (normed * gain[...]).astype(BF16)
+    cols[z, x, :, width:] = ext
     pl.semaphore_wait(barrier, len(greeted))
 
     def remote(src, dst, send, recv, device):
@@ -162,20 +165,50 @@
     def whole(ref, send, recv):
         return remote(ref, ref, send, recv, partner)
 
-    for p in x_peers:
-        remote(xin.at[x], xin.at[x], xg_send.at[0], xg_recv.at[0], at(z, p, core)).start()
-    xg_all = whole(xin.at[pl.ds(0, XS - 1)], xg_send.at[0], xg_recv.at[0])
-    xg_all.wait_recv()
-    rows[z, 0] = jnp.concatenate([xin[j].astype(F32) for j in range(XS)], axis=0).astype(BF16)
-
-    tiles = full // 128
-    cuts = [tiles * i // PIECES * 128 for i in range(PIECES + 1)]
-    ag_cuts = [pl.ds(cuts[i], cuts[i + 1] - cuts[i]) for i in range(PIECES)]
     sides = ((0, -1), (1, 1))
-
-    def ag_copy(way, sign, s, p, last=0):
-        ref = rows.at[slab_of(sign * s), 0, :, ag_cuts[p]]
-        return remote(ref, ref, ag_send.at[way, last], ag_recv.at[way, s, p], step_to[way])
+    x_to = (at(z, lax.rem(x + 1, XS), core), at(z, lax.rem(x + XS - 1, XS), core))
+    x_from = (lax.rem(x + XS - 1, XS), lax.rem(x + 1, XS))
+    middle = full // 256 * 128
+    halves = (pl.ds(0, middle), pl.ds(middle, full - middle))
+
+    def zg_copy(way, sign, leg, r):
+        d = leg * RADIUS + r
+        ref = cols.at[slab_of(sign * leg * RADIUS), x]
+        if d == half:
+            ref = ref.at[:, halves[way]]
+        to = at(slab_of(-sign * r), x, core)
+        return remote(ref, ref, zg_send.at[way, int(d == half)], zg_recv.at[way, d - 1], to)
+
+    def send_leg(leg, way, sign):
+        for r in range(RADIUS, 0, -1):
+            zg_copy(way, sign, leg, r).start()
+
+    def ways_of(d):
+        return sides[:1] if d in (0, half) else sides
+
+    def spread(d):
+        for way, sign in ways_of(d):
+            for side in range(2):
+                ref = cols.at[slab_of(sign * d), x]
+                remote(ref, ref, xf_send.at[0], xf_recv.at[d, side], x_to[side]).start()
+
+    def relay(d):
+        for side in range(2):
+            count = len(ways_of(d))
+            whole(cols.at[pl.ds(0, count), 0], xf_send.at[0], xf_recv.at[d, side]).wait_recv()
+            for way, sign in ways_of(d):
+                ref = cols.at[slab_of(sign * d), x_from[side], :, halves[side]]
+                remote(ref, ref, xr_send.at[0], xr_recv.at[d], x_to[side]).start()
+
+    def collect(d):
+        count = len(ways_of(d))
+        whole(cols.at[pl.ds(0, count), 0], xr_send.at[0], xr_recv.at[d]).wait_recv()
+        for way, sign in ways_of(d):
+            slab = slab_of(sign * d)
+            rows[slab, 0] = jnp.concatenate(
+                [cols[slab, j].astype(F32) for j in range(XS)], axis=0
+            ).astype(BF16)
+            d2_copy(way, sign, d).start()
 
     def d2_copy(way, sign, s):
         slab = slab_of(sign * s)
@@ -186,20 +219,6 @@
 
     def last_pieces(way):
         return tuple(range(PIECES // 2)) if way == 0 else tuple(range(PIECES // 2, PIECES))
-
-    for p in range(PIECES):
-        for way, sign in sides:
-            ag_copy(way, sign, 0, p).start()
-    d2_copy(0, -1, 0).start()
-
-    def gather_step(s, carry):
-        for p in range(PIECES):
-            for way, sign in sides:
-                ag_copy(way, sign, s - 1, p).wait_recv()
-                ag_copy(way, sign, s, p).start()
-        for way, sign in sides:
-            d2_copy(way, sign, s).start()
-        return carry
 
     nt = (((1,), (1,)), ((), ()))
     quarter = width // 4
@@ -238,25 +257,36 @@
         pair_copy(0, d).start()
         pair_copy(1, d).start()
 
-    lax.fori_loop(1, half - 1, gather_step, 0)
-    for p in range(PIECES):
-        for way, sign in sides:
-            ag_copy(way, sign, half - 2, p).wait_recv()
-            if p in last_pieces(way):
-                ag_copy(way, sign, half - 1, p, 1).start()
     for way, sign in sides:
-        d2_copy(way, sign, half - 1).start()
+        send_leg(0, way, sign)
+    spread(0)
+    relay(0)
+    legs = half // RADIUS
+    waiting = [0]
+    for leg in range(legs):
+        near = leg * RADIUS
+        landed = [near + r for r in range(RADIUS, 0, -1)]
+        for d in landed:
+            for way, sign in sides:
+                zg_copy(way, sign, leg, d - near).wait_recv()
+                if d == near + RADIUS and leg < legs - 1:
+                    send_leg(leg + 1, way, sign)
+            spread(d)
+        for d in waiting:
+            collect(d)
+        for d in landed:
+            relay(d)
+        waiting = landed
     for copy in w_copies:
         copy.wait()
     next_rows(half - 2)
-    for way, sign in sides:
-        for p in last_pieces(way):
-            ag_copy(way, sign, half - 1, p).wait_recv()
-    d2_copy(0, -1, half).start()
-    next_rows(half - 1)
+    for d in waiting:
+        collect(d)
+    next_rows(half - 3)
     d2_wait(half, 1)
     expert_rows([half])
     pair_copy(0, half).start()
+    next_rows(half - 1)
 
     def rs_copy(way, d, p, last=0):
         cut = pl.ds(p * piece, piece)
@@ -287,7 +317,6 @@
             ring_out[way, half - 1, :, cut] = local_sum(slab_of(half), p).astype(BF16)
             rs_copy(way, half, p, 1).start()
     pair_wait(half - 1, 2)
-    next_rows(half - 3)
     pass_on(half - 1, lambda way, p: p in last_pieces(way))
 
     def sum_step(i, carry):
@@ -326,12 +355,12 @@
             r = d * NEW + t
             out_ref[t, d : d + 1, :] = result[r : r + 1].astype(BF16)
 
-    xg_all.wait_send()
     xs_all.wait_send()
+    whole(cols.at[:, pl.ds(0, 2)], xf_send.at[0], xf_recv.at[0, 0]).wait_send()
+    whole(cols.at[:, 0], xr_send.at[0], xr_recv.at[0]).wait_send()
     for way in range(2):
-        part = pl.ds(cuts[last_pieces(way)[0]], cuts[last_pieces(way)[-1] + 1] - cuts[last_pieces(way)[0]])
-        whole(rows.at[pl.ds(0, half - 1), 0], ag_send.at[way, 0], ag_recv.at[0, 0, 0]).wait_send()
-        whole(rows.at[0, 0, :, part], ag_send.at[way, 1], ag_recv.at[0, 0, 0]).wait_send()
+        whole(cols.at[pl.ds(0, half - 1), 0], zg_send.at[way, 0], zg_recv.at[0, 0]).wait_send()
+        whole(cols.at[0, 0, :, halves[way]], zg_send.at[way, 1], zg_recv.at[0, 0]).wait_send()
         whole(ring_out.at[0, pl.ds(0, half - 1)], rs_send.at[way, 0], rs_recv.at[0, 0, 0]).wait_send()
         whole(
             ring_out.at[0, 0, :, pl.ds(0, width // 2)], rs_send.at[way, 1], rs_recv.at[0, 0, 0]
@@ -373,7 +402,7 @@
             pltpu.VMEM((hidden, width), BF16),
             pltpu.VMEM((hidden, width), BF16),
             pltpu.VMEM((ROWS, width), F32),
-            pltpu.VMEM((XS, ROWS, full), BF16),
+            pltpu.VMEM((nz, XS, ROWS, full), BF16),
             pltpu.VMEM((nz, 2, class_rows, full), BF16),
             pltpu.VMEM((nz, class_rows, width), F32),
             pltpu.VMEM((nz, class_rows, width), BF16),
@@ -383,8 +412,9 @@
             pltpu.VMEM((XS, ROWS, width), BF16),
             pltpu.VMEM((XS - 1, ROWS, width), BF16),
             dma((5,)), dma((docs, 2)), dma((3,)),
-            dma((1,)), dma((1,)),
-            dma((2, 2)), dma((2, half, PIECES)),
+            dma((2, 2)), dma((2, half)),
+            dma((1,)), dma((half + 1, 2)),
+            dma((1,)), dma((half + 1,)),
             dma((1,)), dma((half + 1,)),
             dma((1,)), dma((half + 1,)),
             dma((2, 2)), dma((2, half, PIECES)),

time: 102 us -> 97.7 us (0.958)
  Pallas kernels: 100 us -> 96.1 us
    pallas_call x1, Pallas kernels: 100 us -> 96.1 us  [per_device(): pl.pallas_call(functools.partial(layer_kernel, nz), name='layer', out_sha...]
where the time goes in v4:
time: 97.7 us; the launch traced here: 97.5 us
  Pallas kernels  96.1 us (98%)
  local copies, waits for them, and re-layouts  1.4 us (1%)
    pallas_call x1, Pallas kernels, per_device(): pl.pallas_call(functools.partial(layer_kernel, nz), name='layer', out_sha...  96.1 us

profile of v4, /device:TPU:40, one launch (start us, length us, event | category | flops | bytes accessed | tf_op | source)
XLA Modules:
  0.0 97.5 jit_solution(17616986889579841865)
XLA Ops:
  0.0 96.1 %layer.1 = bf16[2,2,4096]{2,1,0:T(2,128)(2,1)} custom-call(bf16[2,2,4096]{2,1,0:T(2,128)(2,1)} %hid_hbm.1, f32[1,4096]{1,0:T(1,128)} %bitcast.1, bf16[2,2,4096]{2,1,0:T(2,128)(2,1)} %q_hbm.1, bf16[2,2,1024]{2,1,0:T(2,128)(2,1)} %nk_hbm.1, bf16[2,2,1024]{2,1,0:T(2,128)(2,1)} %nv_hbm.1, bf16[2,384,1024]{2,1,0:T(8,128)(2,1)} %ck_hbm.1, ...), custom_call_target="tpu_custom_call" | custom-call | tf_op jit(solution)/shard_map/layer/pallas_call | solution.py:387
  96.1 1.4 %copy.15 = bf16[2,2,4096]{2,1,0:T(2,128)(2,1)} copy(bf16[2,2,4096]{2,1,0:T(2,128)(2,1)} %layer.1) | data formatting | bytes 65536

commit v5 on v4

--- a/solution.py
+++ b/solution.py
@@ -18,7 +18,6 @@
 TAIL = 128
 XS = 4
 RADIUS = 2
-PIECES = 4
 CORES = 2
 MESH = pl.DeviceIdType.MESH
 F32 = jnp.float32
@@ -29,9 +28,9 @@
     nz, hid_hbm, gain_hbm, q_hbm, nk_hbm, nv_hbm, ck_hbm, cv_hbm, len_ref, routes_ref, logits_ref,
     wg_hbm, wu_hbm, wd_hbm, out_ref,
     hid, gain, q, nk, nv, kbuf, vbuf, wg, wu, wd, carried_ref,
-    cols, rows, mine, pair_out, pair_in, ring_out, ring_in, xs_out, xs_in,
+    cols, rows, mine, pair_out, pair_in, quad, far_out, far_in, near_out, near_in, z_out, z_in,
     in_sems, kv_sems, w_sems, zg_send, zg_recv, xf_send, xf_recv, xr_send, xr_recv, d2_send, d2_recv,
-    pr_send, pr_recv, rs_send, rs_recv, xs_send, xs_recv,
+    pr_send, pr_recv, far_send, far_recv, near_send, near_recv, zs_send, zs_recv,
 ):
     me = lax.axis_index("dp")
     core = me % CORES
@@ -52,11 +51,11 @@
         return lax.rem(z + offset + nz, nz)
 
     partner = at(z, x, 1 - core)
-    step_to = (at(slab_of(1), x, core), at(slab_of(-1), x, core))
-    x_peers = [lax.rem(x + k, XS) for k in range(1, XS)]
+    x_next = (lax.rem(x + 1, XS), lax.rem(x + XS - 1, XS))
+    x_far = lax.rem(x + 2, XS)
 
     barrier = pltpu.get_barrier_semaphore()
-    greeted = [partner] + [at(z, p, core) for p in x_peers]
+    greeted = [partner] + [at(z, p, core) for p in x_next]
     for r in range(1, RADIUS + 1):
         greeted += [at(slab_of(r), x, core), at(slab_of(-r), x, core)]
     for device in greeted:
@@ -166,8 +165,8 @@
         return remote(ref, ref, send, recv, partner)
 
     sides = ((0, -1), (1, 1))
-    x_to = (at(z, lax.rem(x + 1, XS), core), at(z, lax.rem(x + XS - 1, XS), core))
-    x_from = (lax.rem(x + XS - 1, XS), lax.rem(x + 1, XS))
+    x_to = tuple(at(z, p, core) for p in x_next)
+    x_from = x_next[::-1]
     middle = full // 256 * 128
     halves = (pl.ds(0, middle), pl.ds(middle, full - middle))
 
@@ -217,12 +216,10 @@
     def d2_wait(s, count):
         whole(rows.at[pl.ds(0, count), 1], d2_send.at[0], d2_recv.at[s]).wait_recv()
 
-    def last_pieces(way):
-        return tuple(range(PIECES // 2)) if way == 0 else tuple(range(PIECES // 2, PIECES))
-
     nt = (((1,), (1,)), ((), ()))
     quarter = width // 4
-    piece = width // PIECES
+    parts_of = (slice(0, width // 2), slice(width // 2, width))
+    spans_of = (pl.ds(0, width // 2), pl.ds(width // 2, width // 2))
 
     def expert_rows(offsets):
         slabs = [slab_of(o) for o in offsets]
@@ -283,88 +280,127 @@
     for d in waiting:
         collect(d)
     next_rows(half - 3)
-    d2_wait(half, 1)
-    expert_rows([half])
-    pair_copy(0, half).start()
+
+    def local_sum(d):
+        pair_wait(d, len(ways_of(d)))
+        for way, sign in ways_of(d):
+            slab = slab_of(sign * d)
+            total = mine[slab] + pair_in[slab].astype(F32)
+            for j in range(XS):
+                quad[slab, j] = total[j * ROWS : (j + 1) * ROWS]
+            far_out[slab] = quad[slab, x_far].astype(BF16)
+            for side in range(2):
+                remote(
+                    far_out.at[slab, :, spans_of[side]], far_in.at[slab, side],
+                    far_send.at[0], far_recv.at[d], x_to[side],
+                ).start()
+
+    def neighbour_sum(d):
+        count = len(ways_of(d))
+        whole(far_out.at[pl.ds(0, count)], far_send.at[0], far_recv.at[d]).wait_recv()
+        for way, sign in ways_of(d):
+            slab = slab_of(sign * d)
+            for side in range(2):
+                col = x_next[side]
+                here, there = parts_of[side], parts_of[1 - side]
+                near_out[slab, side, :, here] = (
+                    quad[slab, col, :, here] + far_in[slab, side].astype(F32)
+                ).astype(BF16)
+                near_out[slab, side, :, there] = quad[slab, col, :, there].astype(BF16)
+                remote(
+                    near_out.at[slab, side], near_in.at[slab, side],
+                    near_send.at[0], near_recv.at[d], x_to[side],
+                ).start()
+
+    def zs_copy(way, sign, d):
+        src, dst = z_out.at[way, d - 1], z_in.at[way, d - 1]
+        if d == half:
+            src, dst = src.at[:, spans_of[way]], dst.at[:, spans_of[way]]
+        hop = d - (d - 1) // RADIUS * RADIUS
+        to = at(slab_of(sign * hop), x, core)
+        return remote(src, dst, zs_send.at[way, int(d == half)], zs_recv.at[way, d - 1], to)
+
+    def column_sum(d):
+        count = 2 * len(ways_of(d))
+        whole(z_out.at[0, pl.ds(0, count)], near_send.at[0], near_recv.at[d]).wait_recv()
+        for way, sign in ways_of(d):
+            slab = slab_of(sign * d)
+            taken = []
+            if d % RADIUS == 0 and d < half:
+                taken = [(w, s, d + r) for w, s in (sides if d == 0 else ((way, sign),)) for r in range(1, RADIUS + 1)]
+            for w, s, e in taken:
+                zs_copy(w, s, e).wait_recv()
+            sums = []
+            for h in range(2):
+                cut = parts_of[h]
+                total = quad[slab, x, :, cut]
+                for side in range(2):
+                    total = total + near_in[slab, side, :, cut].astype(F32)
+                for w, s, e in taken:
+                    if e < half or h == w:
+                        total = total + z_in[w, e - 1, :, cut].astype(F32)
+                sums.append(total)
+            if d == 0:
+                return jnp.concatenate(sums, axis=1)
+            for w, s in sides if d == half else ((way, sign),):
+                for h in range(2):
+                    if d < half or h == w:
+                        z_out[w, d - 1, :, parts_of[h]] = sums[h].astype(BF16)
+                zs_copy(w, s, d).start()
+
+    def last_rows(d):
+        d2_wait(d, 1)
+        expert_rows([d])
+        pair_copy(0, d).start()
+
+    last_rows(half)
     next_rows(half - 1)
-
-    def rs_copy(way, d, p, last=0):
-        cut = pl.ds(p * piece, piece)
-        return remote(
-            ring_out.at[way, d - 1, :, cut], ring_in.at[way, d - 1, :, cut],
-            rs_send.at[way, last], rs_recv.at[way, d - 1, p], step_to[way],
-        )
-
-    def local_sum(slab, p):
-        cut = slice(p * piece, (p + 1) * piece)
-        return mine[slab, :, cut] + pair_in[slab, :, cut].astype(F32)
-
-    def pass_on(d, has_input):
-        for p in range(PIECES):
-            for way in range(2):
-                cut = slice(p * piece, (p + 1) * piece)
-                total = local_sum(slab_of(d if way == 0 else -d), p)
-                if has_input(way, p):
-                    rs_copy(way, d + 1, p).wait_recv()
-                    total = total + ring_in[way, d, :, cut].astype(F32)
-                ring_out[way, d - 1, :, cut] = total.astype(BF16)
-                rs_copy(way, d, p).start()
-
-    pair_wait(half, 1)
-    for way in range(2):
-        for p in last_pieces(way):
-            cut = slice(p * piece, (p + 1) * piece)
-            ring_out[way, half - 1, :, cut] = local_sum(slab_of(half), p).astype(BF16)
-            rs_copy(way, half, p, 1).start()
-    pair_wait(half - 1, 2)
-    pass_on(half - 1, lambda way, p: p in last_pieces(way))
-
-    def sum_step(i, carry):
-        d = half - 2 - i
-        next_rows(d - 2)
-        pair_wait(d, 2)
-        pass_on(d, lambda way, p: True)
-        return carry
-
-    lax.fori_loop(0, half - 4, sum_step, 0)
-    d2_wait(0, 1)
-    expert_rows([0])
-    pair_copy(0, 0).start()
-    for d in (2, 1):
-        pair_wait(d, 2)
-        pass_on(d, lambda way, p: True)
-
-    pair_wait(0, 1)
-    for p in range(PIECES):
-        cut = slice(p * piece, (p + 1) * piece)
-        total = local_sum(z, p)
-        for way in range(2):
-            rs_copy(way, 1, p).wait_recv()
-            total = total + ring_in[way, 0, :, cut].astype(F32)
-        for j in range(XS):
-            xs_out[j, :, cut] = total[j * ROWS : (j + 1) * ROWS].astype(BF16)
-    for k, p in enumerate(x_peers):
-        remote(xs_out.at[p], xs_in.at[k], xs_send.at[0], xs_recv.at[0], at(z, p, core)).start()
-    result = carried_ref[...] + xs_out[x].astype(F32)
-    xs_all = whole(xs_in, xs_send.at[0], xs_recv.at[0])
-    xs_all.wait_recv()
-    for k in range(XS - 1):
-        result = result + xs_in[k].astype(F32)
+    local_sum(half)
+    next_rows(half - 4)
+    local_sum(half - 1)
+    neighbour_sum(half)
+    local_sum(half - 2)
+    next_rows(half - 5)
+    neighbour_sum(half - 1)
+    column_sum(half)
+    local_sum(half - 3)
+    next_rows(half - 6)
+    neighbour_sum(half - 2)
+    column_sum(half - 1)
+    local_sum(half - 4)
+    next_rows(half - 7)
+    neighbour_sum(half - 3)
+    local_sum(half - 5)
+    last_rows(0)
+    neighbour_sum(half - 4)
+    column_sum(half - 3)
+    local_sum(half - 6)
+    neighbour_sum(half - 5)
+    column_sum(half - 2)
+    local_sum(half - 7)
+    neighbour_sum(half - 6)
+    column_sum(half - 5)
+    local_sum(0)
+    neighbour_sum(half - 7)
+    column_sum(half - 4)
+    neighbour_sum(0)
+    column_sum(half - 7)
+    column_sum(half - 6)
+    result = carried_ref[...] + column_sum(0)
     for d in range(DOC_DEV):
         for t in range(NEW):
             r = d * NEW + t
             out_ref[t, d : d + 1, :] = result[r : r + 1].astype(BF16)
 
-    xs_all.wait_send()
     whole(cols.at[:, pl.ds(0, 2)], xf_send.at[0], xf_recv.at[0, 0]).wait_send()
     whole(cols.at[:, 0], xr_send.at[0], xr_recv.at[0]).wait_send()
     for way in range(2):
         whole(cols.at[pl.ds(0, half - 1), 0], zg_send.at[way, 0], zg_recv.at[0, 0]).wait_send()
         whole(cols.at[0, 0, :, halves[way]], zg_send.at[way, 1], zg_recv.at[0, 0]).wait_send()
-        whole(ring_out.at[0, pl.ds(0, half - 1)], rs_send.at[way, 0], rs_recv.at[0, 0, 0]).wait_send()
-        whole(
-            ring_out.at[0, 0, :, pl.ds(0, width // 2)], rs_send.at[way, 1], rs_recv.at[0, 0, 0]
-        ).wait_send()
+        whole(z_out.at[0, pl.ds(0, half - 1)], zs_send.at[way, 0], zs_recv.at[0, 0]).wait_send()
+        whole(z_out.at[0, 0, :, spans_of[way]], zs_send.at[way, 1], zs_recv.at[0, 0]).wait_send()
+    whole(far_out, far_send.at[0], far_recv.at[0]).wait_send()
+    whole(near_out, near_send.at[0], near_recv.at[0]).wait_send()
     whole(rows.at[:, 0], d2_send.at[0], d2_recv.at[0]).wait_send()
     whole(pair_out, pr_send.at[0], pr_recv.at[0]).wait_send()
 
@@ -407,18 +443,22 @@
             pltpu.VMEM((nz, class_rows, width), F32),
             pltpu.VMEM((nz, class_rows, width), BF16),
             pltpu.VMEM((nz, class_rows, width), BF16),
-            pltpu.VMEM((2, half, class_rows, width), BF16),
-            pltpu.VMEM((2, half, class_rows, width), BF16),
-            pltpu.VMEM((XS, ROWS, width), BF16),
-            pltpu.VMEM((XS - 1, ROWS, width), BF16),
+            pltpu.VMEM((nz, XS, ROWS, width), F32),
+            pltpu.VMEM((nz, ROWS, width), BF16),
+            pltpu.VMEM((nz, 2, ROWS, width // 2), BF16),
+            pltpu.VMEM((nz, 2, ROWS, width), BF16),
+            pltpu.VMEM((nz, 2, ROWS, width), BF16),
+            pltpu.VMEM((2, half, ROWS, width), BF16),
+            pltpu.VMEM((2, half, ROWS, width), BF16),
             dma((5,)), dma((docs, 2)), dma((3,)),
             dma((2, 2)), dma((2, half)),
             dma((1,)), dma((half + 1, 2)),
             dma((1,)), dma((half + 1,)),
             dma((1,)), dma((half + 1,)),
             dma((1,)), dma((half + 1,)),
-            dma((2, 2)), dma((2, half, PIECES)),
-            dma((1,)), dma((1,)),
+            dma((1,)), dma((half + 1,)),
+            dma((1,)), dma((half + 1,)),
+            dma((2, 2)), dma((2, half)),
         ],
         compiler_params=pltpu.CompilerParams(
             collective_id=0, has_side_effects=True, vmem_limit_bytes=56 * 1024 * 1024

time: 97.7 us -> 94.3 us (0.965)
  Pallas kernels: 96.1 us -> 92.7 us
    pallas_call x1, Pallas kernels: 96.1 us -> 92.7 us  [per_device(): pl.pallas_call(functools.partial(layer_kernel, nz), name='layer', out_sha...]
where the time goes in v5:
time: 94.3 us; the launch traced here: 94.1 us
  Pallas kernels  92.7 us (98%)
  local copies, waits for them, and re-layouts  1.4 us (1%)
    pallas_call x1, Pallas kernels, per_device(): pl.pallas_call(functools.partial(layer_kernel, nz), name='layer', out_sha...  92.7 us

profile of v5, /device:TPU:40, one launch (start us, length us, event | category | flops | bytes accessed | tf_op | source)
XLA Modules:
  0.0 94.1 jit_solution(16460035060949250932)
XLA Ops:
  0.0 92.7 %layer.1 = bf16[2,2,4096]{2,1,0:T(2,128)(2,1)} custom-call(bf16[2,2,4096]{2,1,0:T(2,128)(2,1)} %hid_hbm.1, f32[1,4096]{1,0:T(1,128)} %bitcast.1, bf16[2,2,4096]{2,1,0:T(2,128)(2,1)} %q_hbm.1, bf16[2,2,1024]{2,1,0:T(2,128)(2,1)} %nk_hbm.1, bf16[2,2,1024]{2,1,0:T(2,128)(2,1)} %nv_hbm.1, bf16[2,384,1024]{2,1,0:T(8,128)(2,1)} %ck_hbm.1, ...), custom_call_target="tpu_custom_call" | custom-call | tf_op jit(solution)/shard_map/layer/pallas_call | solution.py:423
  92.7 1.4 %copy.15 = bf16[2,2,4096]{2,1,0:T(2,128)(2,1)} copy(bf16[2,2,4096]{2,1,0:T(2,128)(2,1)} %layer.1) | data formatting | bytes 65536

commit v6 on v5

--- a/solution.py
+++ b/solution.py
@@ -18,6 +18,7 @@
 TAIL = 128
 XS = 4
 RADIUS = 2
+BACK = 4
 CORES = 2
 MESH = pl.DeviceIdType.MESH
 F32 = jnp.float32
@@ -56,7 +57,7 @@
 
     barrier = pltpu.get_barrier_semaphore()
     greeted = [partner] + [at(z, p, core) for p in x_next]
-    for r in range(1, RADIUS + 1):
+    for r in range(1, max(RADIUS, BACK) + 1):
         greeted += [at(slab_of(r), x, core), at(slab_of(-r), x, core)]
     for device in greeted:
         pl.semaphore_signal(barrier, inc=1, device_id=device, device_id_type=MESH)
@@ -273,9 +274,15 @@
             collect(d)
         for d in landed:
             relay(d)
+        if leg == 1:
+            for copy in w_copies:
+                copy.wait()
+            d2_wait(0, 1)
+            expert_rows([0])
+            pair_copy(0, 0).start()
+        elif leg > 1:
+            next_rows(near - RADIUS)
         waiting = landed
-    for copy in w_copies:
-        copy.wait()
     next_rows(half - 2)
     for d in waiting:
         collect(d)
@@ -316,7 +323,7 @@
         src, dst = z_out.at[way, d - 1], z_in.at[way, d - 1]
         if d == half:
             src, dst = src.at[:, spans_of[way]], dst.at[:, spans_of[way]]
-        hop = d - (d - 1) // RADIUS * RADIUS
+        hop = d - (d - 1) // BACK * BACK
         to = at(slab_of(sign * hop), x, core)
         return remote(src, dst, zs_send.at[way, int(d == half)], zs_recv.at[way, d - 1], to)
 
@@ -326,8 +333,8 @@
         for way, sign in ways_of(d):
             slab = slab_of(sign * d)
             taken = []
-            if d % RADIUS == 0 and d < half:
-                taken = [(w, s, d + r) for w, s in (sides if d == 0 else ((way, sign),)) for r in range(1, RADIUS + 1)]
+            if d % BACK == 0 and d < half:
+                taken = [(w, s, d + r) for w, s in (sides if d == 0 else ((way, sign),)) for r in range(1, BACK + 1)]
             for w, s, e in taken:
                 zs_copy(w, s, e).wait_recv()
             sums = []
@@ -353,39 +360,36 @@
         expert_rows([d])
         pair_copy(0, d).start()
 
+    local_sum(half - 2)
     last_rows(half)
+    local_sum(half - 3)
     next_rows(half - 1)
     local_sum(half)
-    next_rows(half - 4)
+    neighbour_sum(half - 2)
     local_sum(half - 1)
+    neighbour_sum(half - 3)
+    local_sum(half - 4)
     neighbour_sum(half)
-    local_sum(half - 2)
+    column_sum(half - 2)
     next_rows(half - 5)
     neighbour_sum(half - 1)
+    column_sum(half - 3)
+    local_sum(half - 5)
+    neighbour_sum(half - 4)
     column_sum(half)
-    local_sum(half - 3)
-    next_rows(half - 6)
-    neighbour_sum(half - 2)
-    column_sum(half - 1)
-    local_sum(half - 4)
     next_rows(half - 7)
-    neighbour_sum(half - 3)
-    local_sum(half - 5)
-    last_rows(0)
-    neighbour_sum(half - 4)
-    column_sum(half - 3)
     local_sum(half - 6)
     neighbour_sum(half - 5)
-    column_sum(half - 2)
+    column_sum(half - 1)
     local_sum(half - 7)
     neighbour_sum(half - 6)
+    local_sum(0)
+    column_sum(half - 4)
+    neighbour_sum(half - 7)
     column_sum(half - 5)
-    local_sum(0)
-    neighbour_sum(half - 7)
-    column_sum(half - 4)
     neighbour_sum(0)
+    column_sum(half - 6)
     column_sum(half - 7)
-    column_sum(half - 6)
     result = carried_ref[...] + column_sum(0)
     for d in range(DOC_DEV):
         for t in range(NEW):

time: 94.3 us -> 91.6 us (0.971)
  Pallas kernels: 92.7 us -> 89.2 us
    pallas_call x1, Pallas kernels: 92.7 us -> 89.2 us  [per_device(): pl.pallas_call(functools.partial(layer_kernel, nz), name='layer', out_sha...]
where the time goes in v6:
time: 91.6 us; the launch traced here: 90.6 us
  Pallas kernels  89.2 us (97%)
  local copies, waits for them, and re-layouts  1.4 us (2%)
    pallas_call x1, Pallas kernels, per_device(): pl.pallas_call(functools.partial(layer_kernel, nz), name='layer', out_sha...  89.2 us

profile of v6, /device:TPU:40, one launch (start us, length us, event | category | flops | bytes accessed | tf_op | source)
XLA Modules:
  0.0 90.6 jit_solution(11083851621742274804)
XLA Ops:
  0.0 89.2 %layer.1 = bf16[2,2,4096]{2,1,0:T(2,128)(2,1)} custom-call(bf16[2,2,4096]{2,1,0:T(2,128)(2,1)} %hid_hbm.1, f32[1,4096]{1,0:T(1,128)} %bitcast.1, bf16[2,2,4096]{2,1,0:T(2,128)(2,1)} %q_hbm.1, bf16[2,2,1024]{2,1,0:T(2,128)(2,1)} %nk_hbm.1, bf16[2,2,1024]{2,1,0:T(2,128)(2,1)} %nv_hbm.1, bf16[2,384,1024]{2,1,0:T(8,128)(2,1)} %ck_hbm.1, ...), custom_call_target="tpu_custom_call" | custom-call | tf_op jit(solution)/shard_map/layer/pallas_call | solution.py:427
  89.2 1.4 %copy.15 = bf16[2,2,4096]{2,1,0:T(2,128)(2,1)} copy(bf16[2,2,4096]{2,1,0:T(2,128)(2,1)} %layer.1) | data formatting | bytes 65536
